TPU v7x, 32 devices: a 4x4x1 block of a 4x4x8 slice. The times are simulated.
32 devices in a mesh: dp: 1 (over z), tp: 4 (over y), sp: 8 (over x, core).
Axes of the slice: x: 4, y: 4, z: 1, core: 2. Of those that a mesh axis runs over, the one named last changes fastest.
The devices are a block of a 4x4x8 slice.
Arguments:
- hidden: bfloat16 [256, 7168], P('dp')
- lat_cache: bfloat16 [256, 2048, 512], P('dp', 'sp')
- rope_cache: bfloat16 [256, 2048, 64], P('dp', 'sp')
- positions: int32 [256], P('dp')
- w_dq: bfloat16 [7168, 1536], replicated
- gain_q: bfloat16 [1536], replicated
- w_dkv: bfloat16 [7168, 576], replicated
- gain_kv: bfloat16 [512], replicated
- w_uq: bfloat16 [1536, 64, 192], P(None, 'tp')
- w_uk: bfloat16 [512, 64, 128], P(None, 'tp')
- w_uv: bfloat16 [512, 64, 128], P(None, 'tp')
- w_out: bfloat16 [8192, 7168], P('tp')
Outputs:
- output 1: bfloat16 [256, 7168], P('dp')
- output 2: bfloat16 [256, 2048, 512], P('dp', 'sp')
- output 3: bfloat16 [256, 2048, 64], P('dp', 'sp')
All inputs are finite; a program needn't handle non-finite values.
Results may differ from a plain program's by a relative error of at most 0.0115735.
Values sent between devices are 32-bit elements.
A program may use at most 768 MiB of HBM per device.

v0:
```python
import math
import jax
import jax.numpy as jnp
from jax import lax
from jax.sharding import PartitionSpec as P

EPSILON = 1e-6
ROPE_BASE = 50000.0
YARN_MSCALE = 1.0 + 0.1 * math.log(32.0)
MASK_VALUE = -1e30


def rms_norm(values, gain):
    vals32 = values.astype(jnp.float32)
    inv_rms = lax.rsqrt(jnp.mean(vals32 * vals32, axis=-1, keepdims=True) + EPSILON)
    return vals32 * inv_rms * gain.astype(jnp.float32)


def rope_tables(positions, rope_dim):
    half_dim = rope_dim // 2
    inv_freq = ROPE_BASE ** (-jnp.arange(half_dim).astype(jnp.float32) / half_dim)
    angles = positions.astype(jnp.float32)[:, None] * inv_freq[None, :]
    return jnp.cos(angles), jnp.sin(angles)


def rotate_pairs(values, cos_t, sin_t):
    half_dim = values.shape[-1] // 2
    first_half = values[..., :half_dim]
    second_half = values[..., half_dim:]
    return jnp.concatenate([first_half * cos_t - second_half * sin_t, second_half * cos_t + first_half * sin_t], axis=-1)


def project_inputs(hidden, positions, w_dq, gain_q, w_dkv, gain_kv, w_uq, w_uk):
    kv_rank = w_uk.shape[0]
    nope_dim = w_uk.shape[2]
    cos_t, sin_t = rope_tables(positions, w_uq.shape[2] - nope_dim)
    h_q = jnp.dot(hidden, w_dq, preferred_element_type=jnp.float32).astype(jnp.bfloat16)
    c_q = rms_norm(h_q, gain_q).astype(jnp.bfloat16)
    q_full = jnp.einsum('br,rhd->bhd', c_q, w_uq, preferred_element_type=jnp.float32).astype(jnp.bfloat16)
    q_rope = rotate_pairs(q_full[:, :, nope_dim:].astype(jnp.float32), cos_t[:, None, :], sin_t[:, None, :]).astype(jnp.bfloat16)
    q_abs = jnp.einsum('bhn,khn->bhk', q_full[:, :, :nope_dim], w_uk, preferred_element_type=jnp.float32).astype(jnp.bfloat16)
    kv_down = jnp.dot(hidden, w_dkv, preferred_element_type=jnp.float32).astype(jnp.bfloat16)
    lat_new = rms_norm(kv_down[:, :kv_rank], gain_kv).astype(jnp.bfloat16)
    rope_new = rotate_pairs(kv_down[:, kv_rank:].astype(jnp.float32), cos_t, sin_t).astype(jnp.bfloat16)
    return q_abs, q_rope, lat_new, rope_new


def solution(mesh):
    row_spec = P('dp', None)
    cache_spec = P('dp', 'sp', None)
    head_spec = P(None, 'tp', None)
    in_specs = (row_spec, cache_spec, cache_spec, P('dp'), P(), P(), P(), P(), head_spec, head_spec, head_spec, P('tp', None))
    out_specs = (row_spec, cache_spec, cache_spec)

    def local_step(hidden, lat_cache, rope_cache, positions, w_dq, gain_q, w_dkv, gain_kv, w_uq, w_uk, w_uv, w_out):
        rows_local = hidden.shape[0]
        seq_local = lat_cache.shape[1]
        score_scale = YARN_MSCALE ** 2 / math.sqrt(w_uq.shape[2])
        q_abs, q_rope, lat_new, rope_new = project_inputs(hidden, positions, w_dq, gain_q, w_dkv, gain_kv, w_uq, w_uk)
        slot_ids = lax.axis_index('sp') * seq_local + jnp.arange(seq_local)
        slot_hit = (slot_ids[None, :] == positions[:, None])[:, :, None]
        lat_all = jnp.where(slot_hit, lat_new[:, None, :], lat_cache)
        rope_all = jnp.where(slot_hit, rope_new[:, None, :], rope_cache)
        scores = (jnp.einsum('bhk,bsk->bhs', q_abs, lat_all, preferred_element_type=jnp.float32) + jnp.einsum('bhr,bsr->bhs', q_rope, rope_all, preferred_element_type=jnp.float32)) * score_scale
        key_valid = slot_ids[None, None, :] <= positions[:, None, None]
        scores = jnp.where(key_valid, scores, MASK_VALUE)
        max_global = lax.pmax(jnp.max(scores, axis=-1), 'sp')
        weights = jnp.exp(scores - max_global[:, :, None])
        lat_part = jnp.einsum('bhs,bsk->bhk', weights.astype(jnp.bfloat16), lat_all, preferred_element_type=jnp.float32)
        denominator, lat_sum = lax.psum((jnp.sum(weights, axis=-1), lat_part), 'sp')
        o_lat = (lat_sum / denominator[:, :, None]).astype(jnp.bfloat16)
        o_heads = jnp.einsum('bhk,khv->bhv', o_lat, w_uv, preferred_element_type=jnp.float32).astype(jnp.bfloat16)
        attn_part = jnp.dot(o_heads.reshape(rows_local, -1), w_out, preferred_element_type=jnp.float32)
        attn_out = lax.psum(attn_part, 'tp')
        return (hidden.astype(jnp.float32) + attn_out).astype(jnp.bfloat16), lat_all, rope_all

    return jax.shard_map(local_step, mesh=mesh, in_specs=in_specs, out_specs=out_specs, check_vma=False)
```

profile of v0, /device:TPU:102, one launch (start us, length us, event | category | flops | bytes accessed | tf_op | source)
XLA Modules:
  0.0 469.0 jit_solution(7793635839557545070)
XLA Ops:
  7.2 0.0 copy-start
  7.2 0.1 all-reduce.3.cloned.1.call-start
  7.3 0.0 copy-start.4
  7.3 0.0 copy-start.6
  7.3 0.0 copy-start.5
  7.3 6.9 %convolution_convert_fusion.1 = bf16[256,576]{0,1:T(8,128)(2,1)S(1)} fusion(bf16[256,7168]{1,0:T(8,128)(2,1)} %param.12, bf16[7168,576]{0,1:T(8,128)(2,1)} %param.18), kind=kOutput, calls=%fused_computation.22 | convolution fusion | flops 2114076672 | bytes 12222464 | tf_op jit(solution)/shard_map/dot_general | solution.py:42
  14.2 0.1 fusion.20
  14.3 0.0 copy-done.4
  14.4 0.0 copy-done.6
  14.4 0.0 copy-done.5
  14.4 0.1 broadcast_compare_fusion.1
  14.6 0.1 fusion.22
  14.7 0.1 copy.19
  14.9 0.2 subtract_convert_fusion.1
  15.1 0.1 copy.20
  15.2 11.7 %multiply_reduce_fusion = (f32[256]{0:T(256)S(1)}, f32[256,1536]{1,0:T(8,128)S(1)}) fusion(bf16[256,7168]{1,0:T(8,128)(2,1)} %param.12, bf16[7168,1536]{1,0:T(8,128)(2,1)} %param.16), kind=kOutput, calls=%fused_computation.20 | convolution fusion | flops 5638717440 | bytes 27264000 | tf_op jit(solution)/shard_map/dot_general | solution.py:37
  27.0 5.4 %fusion.17 = f32[256,3072]{0,1:S(1)} fusion(bf16[1536,3072]{0,1:T(8,128)(2,1)} %bitcast.21, f32[256,1536]{1,0:T(8,128)S(1)} %get-tuple-element.12, f32[1536]{0:T(1024)S(1)} %convert_element_type.76, f32[256]{0:T(256)S(1)} %add_rsqrt_fusion.1), kind=kOutput, calls=%fused_computation.24 | convolution fusion | flops 2417098752 | bytes 14162944
  32.4 0.2 convert_element_type.78
  32.6 0.0 copy-start.2
  32.6 1.1 copy-done.2
  33.7 0.1 slice_convert_fusion
  33.8 0.2 subtract_convert_fusion
  34.1 1.9 copy.21
  35.9 0.0 copy-done
  35.9 4.7 %fusion.9 = bf16[16,256,512]{2,1,0:T(8,128)(2,1)} fusion(bf16[512,16,128]{2,1,0:T(8,128)(2,1)S(1)} %copy-done, bf16[256,16,192]{0,2,1:T(8,128)(2,1)} %copy-done.2), kind=kOutput, calls=%fused_computation.15 | convolution fusion | flops 536870912 | bytes 7340032 | tf_op jit(solution)/shard_map/bhn,khn->bhk/dot_general | solution.py:41
  40.6 7.9 %broadcast_select_fusion.1 = bf16[256,256,64]{1,2,0:T(8,128)(2,1)} fusion(bf16[256,256,64]{1,2,0:T(8,128)(2,1)} %param.14, pred[256,256]{1,0:T(8,128)(4,1)S(1)} %get-tuple-element.8, bf16[256,64]{1,0:T(8,128)(2,1)S(1)} %copy.20), kind=kLoop, calls=%fused_computation.3 | loop fusion | flops 4194304 | bytes 16875520 | tf_op jit(solution)/shard_map/jit(_where)/select_n | solution.py:63
  48.5 44.6 %broadcast_select_fusion = bf16[256,256,512]{2,1,0:T(8,128)(2,1)} fusion(bf16[256,256,512]{2,1,0:T(8,128)(2,1)} %param.13, pred[256,256]{1,0:T(8,128)(4,1)S(1)} %get-tuple-element.8, bf16[256,512]{1,0:T(8,128)(2,1)S(1)} %copy.19), kind=kLoop, calls=%fused_computation | loop fusion | flops 33554432 | bytes 134545408 | tf_op jit(solution)/shard_map/jit(_where)/select_n | solution.py:62
  93.1 0.0 copy-start.3
  93.1 26.8 %fusion.1 = f32[256,16,256]{2,1,0:T(8,128)S(1)} fusion(bf16[256,256,512]{2,1,0:T(8,128)(2,1)} %broadcast_select_fusion, bf16[16,256,512]{2,1,0:T(8,128)(2,1)} %fusion.9), kind=kOutput, calls=%fused_computation.6 | convolution fusion | flops 1073741824 | bytes 75497472 | tf_op jit(solution)/shard_map/bhk,bsk->bhs/dot_general | solution.py:64
  119.9 0.0 copy-done.3
  119.9 6.9 %fusion.23 = (f32[256,16]{1,0:T(8,128)S(1)}, f32[256,16,256]{2,1,0:T(8,128)}) fusion(f32[256,16,256]{2,1,0:T(8,128)S(1)} %fusion.1, bf16[256,16,64]{2,1,0:T(8,128)(2,1)S(1)} %copy-done.3, bf16[256,256,64]{1,2,0:T(8,128)(2,1)} %broadcast_select_fusion.1, pred[256,256]{1,0:T(8,128)(4,1)S(1)} %get-tuple-element.7), kind=kOutput, calls=%fused_computation.48 | convolution fusion | flops 138407936 | bytes 17383424 | tf_op jit(solution)/shard_map/bhr,bsr->bhs/dot_general | solution.py:64
  126.9 24.2 %pmax.7 = f32[256,16]{1,0:T(8,128)S(1)} all-reduce(f32[256,16]{1,0:T(8,128)S(1)} %get-tuple-element.13), channel_id=1, replica_groups=mesh['dp'=1,'tp'=4,'sp'=8] {'sp'}, use_global_device_ids=true, to_apply=%region_3.4 | all-reduce | flops 4096 | bytes 32768 | tf_op jit(solution)/shard_map/pmax | solution.py:67
  151.1 28.2 %fusion.7 = f32[256,16,512]{2,1,0:T(8,128)} fusion(bf16[256,256,512]{2,1,0:T(8,128)(2,1)} %broadcast_select_fusion, f32[256,16,256]{2,1,0:T(8,128)} %get-tuple-element.14, f32[256,16]{1,0:T(8,128)S(1)} %pmax.7), kind=kOutput, calls=%fused_computation.14 | convolution fusion | flops 1075838976 | bytes 79708160 | tf_op jit(solution)/shard_map/bhs,bsk->bhk/dot_general | solution.py:69
  179.3 11.5 %copy.26 = f32[256,16,512]{2,0,1:T(8,128)} copy(f32[256,16,512]{2,1,0:T(8,128)} %fusion.7) | data formatting | bytes 16777216 | tf_op jit(solution)/shard_map/bhs,bsk->bhk/dot_general | solution.py:69
  190.7 0.1 all-reduce.3.cloned.1.call-update
  190.8 0.1 all-reduce.5.cloned.1.call-start
  190.9 2.9 fusion.4
  193.8 25.9 %psum.22 = f32[256,16]{1,0:T(8,128)S(1)} all-reduce(f32[256,16]{1,0:T(8,128)S(1)} %fusion.4), channel_id=1, replica_groups=mesh['dp'=1,'tp'=4,'sp'=8] {'sp'}, use_global_device_ids=true, to_apply=%region_6.7 | all-reduce | flops 4096 | bytes 32768 | tf_op jit(solution)/shard_map/psum | solution.py:70
  219.7 0.1 copy.22
  219.7 72.6 %all-reduce.3.cloned.1.call-done = f32[256,16,512]{2,0,1:T(8,128)} async-done(((f32[256,16,512]{2,0,1:T(8,128)}), f32[256,16,512]{2,0,1:T(8,128)}) %all-reduce.3.cloned.1.call-update) | async-done | bytes 8388624 | tf_op jit(solution)/shard_map/psum | solution.py:70
  292.3 5.9 %fusion.13 = bf16[16,256,128]{1,2,0:T(8,128)(2,1)S(1)} fusion(bf16[512,16,128]{2,1,0:T(8,128)(2,1)} %param.22, f32[256,16,512]{2,0,1:T(8,128)} %all-reduce.3.cloned.1.call-done, f32[256,16]{0,1:T(8,128)S(1)} %copy.22), kind=kOutput, calls=%fused_computation.21 | convolution fusion | flops 541589504 | bytes 11550720 | tf_op jit(solution)/shard_map/bhk,khv->bhv/dot_general | solution.py:72
  298.2 16.5 %fusion.24 = f32[256,7168]{1,0:T(8,128)} fusion(bf16[256,2048]{0,1:T(8,128)(2,1)S(1)} %bitcast.20, bf16[2048,7168]{1,0:T(8,128)(2,1)} %param.23), kind=kOutput, calls=%fused_computation.49 | convolution fusion | flops 7516192768 | bytes 37748736 | tf_op jit(solution)/shard_map/dot_general | solution.py:73
  314.6 0.1 all-reduce.5.cloned.1.call-update
  314.7 0.0 copy-start.1
  314.7 140.5 %all-reduce.5.cloned.1.call-done = f32[256,7168]{1,0:T(8,128)} async-done(((f32[256,7168]{1,0:T(8,128)}), f32[256,7168]{1,0:T(8,128)}) %all-reduce.5.cloned.1.call-update) | async-done | bytes 7340048 | tf_op jit(solution)/shard_map/psum | solution.py:74
  455.2 6.9 %add_convert_fusion = bf16[256,7168]{1,0:T(8,128)(2,1)} fusion(f32[256,7168]{1,0:T(8,128)} %all-reduce.5.cloned.1.call-done, bf16[256,7168]{1,0:T(8,128)(2,1)} %param.12), kind=kLoop, calls=%fused_computation.4 | loop fusion | flops 5505024 | bytes 14680064 | tf_op jit(solution)/shard_map/convert_element_type | solution.py:75
  462.1 0.0 copy-done.1
  (10 shorter events, 0.1 us)
Async XLA Ops:
  7.2 28.7 %copy-start = (bf16[512,16,128]{2,1,0:T(8,128)(2,1)S(1)}, bf16[512,16,128]{2,1,0:T(8,128)(2,1)}, u32[]{:S(2)}) copy-start(bf16[512,16,128]{2,1,0:T(8,128)(2,1)} %param.21) | copy-start | bytes 6291460
  7.2 285.1 %all-reduce.3.cloned.1.call-start = ((), (), s32[]{:S(2)}) async-start(), calls=%async_computation | async-start | bytes 16777216 | tf_op jit(solution)/shard_map/psum | solution.py:70
  7.3 7.1 %copy-start.4 = (s32[256]{0:T(256)S(1)}, s32[256]{0:T(256)}, u32[]{:S(2)}) copy-start(s32[256]{0:T(256)} %param.15) | copy-start | bytes 3076
  7.3 7.1 %copy-start.6 = (bf16[512]{0:T(512)(128)(2,1)S(1)}, bf16[512]{0:T(512)(128)(2,1)}, u32[]{:S(2)}) copy-start(bf16[512]{0:T(512)(128)(2,1)} %param.19) | copy-start | bytes 3076
  7.3 7.1 %copy-start.5 = (bf16[1536]{0:T(1024)(128)(2,1)S(1)}, bf16[1536]{0:T(1024)(128)(2,1)}, u32[]{:S(2)}) copy-start(bf16[1536]{0:T(1024)(128)(2,1)} %param.17) | copy-start | bytes 9220
  32.6 1.1 copy-start.2
  93.1 26.8 %copy-start.3 = (bf16[256,16,64]{2,1,0:T(8,128)(2,1)S(1)}, bf16[256,16,64]{2,1,0:T(8,128)(2,1)}, u32[]{:S(2)}) copy-start(bf16[256,16,64]{2,1,0:T(8,128)(2,1)} %copy.21) | copy-start | bytes 1572868
  190.8 264.4 %all-reduce.5.cloned.1.call-start = ((), (), s32[]{:S(2)}) async-start(), calls=%async_computation.1 | async-start | bytes 14680064 | tf_op jit(solution)/shard_map/psum | solution.py:74
  314.7 147.4 %copy-start.1 = (bf16[512,16,128]{2,1,0:T(8,128)(2,1)S(1)}, bf16[512,16,128]{2,1,0:T(8,128)(2,1)}, u32[]{:S(2)}) copy-start(bf16[512,16,128]{2,1,0:T(8,128)(2,1)} %param.21) | copy-start | bytes 6291460
Sparse Core Ops, SparseCore 0:
  190.9 101.3 all-reduce.2
  314.8 140.3 all-reduce.4
where the time goes:
time: 470 us; the launch traced here: 469 us
  waiting for transfers between devices  213 us (45%)
  matrix products  113 us (24%)
  other arithmetic  63.4 us (13%)
  blocking collectives  50.1 us (11%)
  local copies, waits for them, and re-layouts  14.8 us (3%)
  between operations  14.3 us (3%)
    psum x1, waiting for transfers between devices, local_step(): attn_out = lax.psum(attn_part, 'tp')  140 us
    psum x1, waiting for transfers between devices, local_step(): denominator, lat_sum = lax.psum((jnp.sum(weights, axis=-1), lat_part), 'sp')  72.6 us
    select_n x1, other arithmetic, local_step(): lat_all = jnp.where(slot_hit, lat_new[:, None, :], lat_cache)  44.6 us
    dot_general x1, matrix products, local_step(): jnp.einsum('bhs,bsk->bhk', weights.astype(jnp.bfloat16), lat_all, preferr...  28.2 us
    dot_general x1, matrix products, local_step(): jnp.einsum('bhk,bsk->bhs', q_abs, lat_all, preferred_element_type=jnp.flo...  26.8 us
    psum x1, blocking collectives, local_step(): denominator, lat_sum = lax.psum((jnp.sum(weights, axis=-1), lat_part), 'sp')  25.9 us
    pmax x1, blocking collectives, local_step(): max_global = lax.pmax(jnp.max(scores, axis=-1), 'sp')  24.2 us
    dot_general x1, matrix products, local_step(): jnp.dot(o_heads.reshape(rows_local, -1), w_out, preferred_element_type=jn...  16.5 us
  transfers between devices with their start and end apart: 2, of which 2 were waited for; matrix products, arithmetic and copies ran while one was open for 1% of the time, Pallas kernels for 0%

commit v1 on v0

--- a/solution.py
+++ b/solution.py
@@ -1,13 +1,20 @@
+import functools
 import math
 import jax
 import jax.numpy as jnp
 from jax import lax
+from jax.experimental import pallas as pl
+from jax.experimental.pallas import tpu as pltpu
 from jax.sharding import PartitionSpec as P
 
 EPSILON = 1e-6
 ROPE_BASE = 50000.0
 YARN_MSCALE = 1.0 + 0.1 * math.log(32.0)
 MASK_VALUE = -1e30
+CHIPS = 4
+SUBLANES = 8
+LANES = 128
+NT_DIMS = (((1,), (1,)), ((), ()))
 
 
 def rms_norm(values, gain):
@@ -45,33 +52,223 @@
     return q_abs, q_rope, lat_new, rope_new
 
 
+def merge_parts(parts, lane):
+    groups = len(parts[0]) // 4
+    stats = [p[-1] for p in parts]
+    out, maxes, dens = [], [], []
+    for g in range(groups):
+        ms = [jnp.broadcast_to(s[:, 2 * g:2 * g + 1], s.shape) for s in stats]
+        ls = [jnp.broadcast_to(s[:, 2 * g + 1:2 * g + 2], s.shape) for s in stats]
+        top = functools.reduce(jnp.maximum, ms)
+        ws = [jnp.exp(m - top) for m in ms]
+        maxes.append(top)
+        dens.append(sum(w * l for w, l in zip(ws, ls)))
+        for n in range(4):
+            out.append(sum(w * p[4 * g + n] for w, p in zip(ws, parts)))
+    return out, maxes, dens
+
+
+def pack_stats(maxes, dens, lane):
+    tile = jnp.zeros((SUBLANES, LANES), jnp.float32)
+    for g, (m, l) in enumerate(zip(maxes, dens)):
+        tile = jnp.where(lane == 2 * g, m, tile)
+        tile = jnp.where(lane == 2 * g + 1, l, tile)
+    return tile
+
+
+def attend_kernel(rounds, inner, scale, pos_ref, lat_ref, rope_ref, qa_ref, qr_ref, cn_ref, kn_ref, out_ref,
+                  part, peer_in, merged, far_in, relay, dir_in, rel_in,
+                  peer_send, far_send, dir_send, rel_send, peer_recv, far_recv, dir_recv, rel_recv):
+    t = pl.program_id(0)
+    me = lax.axis_index('sp')
+    chip, core = me // 2, lax.rem(me, 2)
+    owners = lat_ref.shape[1]
+    slots = lat_ref.shape[3]
+    heads, rank = qa_ref.shape[3], qa_ref.shape[4]
+    lane = lax.broadcasted_iota(jnp.int32, (SUBLANES, LANES), 1)
+    tiles = part.shape[3]
+
+    def at_chip(index):
+        return {'sp': lax.rem(index + CHIPS, CHIPS) * 2 + core}
+
+    def peer_copy(r):
+        return pltpu.make_async_remote_copy(
+            src_ref=part.at[r, 1 - core], dst_ref=peer_in.at[r], send_sem=peer_send.at[lax.rem(r, 4)], recv_sem=peer_recv.at[r],
+            device_id={'sp': chip * 2 + 1 - core}, device_id_type=pl.DeviceIdType.MESH)
+
+    def direction(r):
+        return 1 - 2 * lax.rem(r, 2)
+
+    def far_copy(r):
+        s = direction(r)
+        return pltpu.make_async_remote_copy(
+            src_ref=merged.at[r, lax.rem(chip + 2, CHIPS)], dst_ref=far_in.at[r], send_sem=far_send.at[lax.rem(r, 4)],
+            recv_sem=far_recv.at[r], device_id=at_chip(chip + s), device_id_type=pl.DeviceIdType.MESH)
+
+    def dir_copy(r):
+        s = direction(r)
+        return pltpu.make_async_remote_copy(
+            src_ref=merged.at[r, lax.rem(chip - s + CHIPS, CHIPS)], dst_ref=dir_in.at[r], send_sem=dir_send.at[lax.rem(r, 4)],
+            recv_sem=dir_recv.at[r], device_id=at_chip(chip - s), device_id_type=pl.DeviceIdType.MESH)
+
+    def rel_copy(r):
+        s = direction(r)
+        return pltpu.make_async_remote_copy(
+            src_ref=relay.at[r], dst_ref=rel_in.at[r], send_sem=rel_send.at[lax.rem(r, 4)],
+            recv_sem=rel_recv.at[r], device_id=at_chip(chip + s), device_id_type=pl.DeviceIdType.MESH)
+
+    @pl.when(t == 0)
+    def _():
+        barrier = pltpu.get_barrier_semaphore()
+        pl.semaphore_signal(barrier, inc=1, device_id={'sp': chip * 2 + 1 - core}, device_id_type=pl.DeviceIdType.MESH)
+        pl.semaphore_signal(barrier, inc=1, device_id=at_chip(chip + 1), device_id_type=pl.DeviceIdType.MESH)
+        pl.semaphore_signal(barrier, inc=1, device_id=at_chip(chip - 1), device_id_type=pl.DeviceIdType.MESH)
+        pl.semaphore_wait(barrier, 3)
+
+    @pl.when(t < rounds)
+    def _():
+        base = me * slots
+        slot = lax.broadcasted_iota(jnp.int32, (heads, slots), 1)
+        scores, news, valid, hits, fresh = [], [], [], [], []
+        for j in range(owners):
+            row = (t // inner) * (owners * inner) + j * inner + lax.rem(t, inner)
+            local = pos_ref[row] - base
+            qa, qr = qa_ref[0, j, 0], qr_ref[0, j, 0]
+            lat_s = lax.dot_general(qa, lat_ref[0, j, 0], NT_DIMS, preferred_element_type=jnp.float32)
+            rope_s = jnp.dot(qr, rope_ref[0, j, 0], preferred_element_type=jnp.float32)
+            c_new = cn_ref[pl.ds(row, 1), :]
+            k_new = kn_ref[pl.ds(row, 1), :]
+            s_new = (jnp.sum(qa.astype(jnp.float32) * c_new, axis=-1, keepdims=True)
+                     + jnp.sum(qr.astype(jnp.float32) * k_new, axis=-1, keepdims=True)) * scale
+            ok = slot < local
+            hit = jnp.full((heads, 1), local, jnp.int32)
+            hit = (hit >= 0) & (hit < slots)
+            scores.append(jnp.where(ok, (lat_s + rope_s) * scale, MASK_VALUE))
+            news.append(jnp.where(hit, s_new, MASK_VALUE))
+            valid.append(ok)
+            hits.append(hit)
+            fresh.append(c_new)
+        for j in range(owners):
+            top = jnp.maximum(jnp.max(scores[j], axis=-1, keepdims=True), news[j])
+            weights = jnp.where(valid[j], jnp.exp(scores[j] - top), 0.0)
+            w_new = jnp.where(hits[j], jnp.exp(news[j] - top), 0.0)
+            den = jnp.sum(weights, axis=-1, keepdims=True) + w_new
+            lat_sum = jnp.dot(weights.astype(jnp.bfloat16), lat_ref[0, j, 0], preferred_element_type=jnp.float32)
+            lat_sum = lat_sum + w_new.astype(jnp.bfloat16).astype(jnp.float32) * fresh[j]
+            for g in range(heads // SUBLANES):
+                for n in range(rank // LANES):
+                    part[t, j % 2, j // 2, 4 * g + n] = lat_sum[SUBLANES * g:SUBLANES * (g + 1), LANES * n:LANES * (n + 1)]
+            split = [slice(SUBLANES * g, SUBLANES * (g + 1)) for g in range(heads // SUBLANES)]
+            part[t, j % 2, j // 2, tiles - 1] = pack_stats([top[g] for g in split], [den[g] for g in split], lane)
+
+    @pl.when((t >= 1) & (t < rounds + 1))
+    def _():
+        r = t - 1
+        peer_copy(r).wait()
+        for d in range(CHIPS):
+            mine = [part[r, core, d, n] for n in range(tiles)]
+            theirs = [peer_in[r, d, n] for n in range(tiles)]
+            out, maxes, dens = merge_parts([mine, theirs], lane)
+            for n in range(tiles - 1):
+                merged[r, d, n] = out[n]
+            merged[r, d, tiles - 1] = pack_stats(maxes, dens, lane)
+
+    @pl.when(t < rounds)
+    def _():
+        peer_copy(t).start()
+
+    @pl.when((t >= 3) & (t < rounds + 3))
+    def _():
+        r = t - 3
+        far_copy(r).wait()
+        d = lax.rem(chip + direction(r) + CHIPS, CHIPS)
+        mine = [merged[r, d, n] for n in range(tiles)]
+        theirs = [far_in[r, n] for n in range(tiles)]
+        out, maxes, dens = merge_parts([mine, theirs], lane)
+        for n in range(tiles - 1):
+            relay[r, n] = out[n]
+        relay[r, tiles - 1] = pack_stats(maxes, dens, lane)
+
+    @pl.when((t >= 1) & (t < rounds + 1))
+    def _():
+        far_copy(t - 1).start()
+        dir_copy(t - 1).start()
+
+    @pl.when(t >= 5)
+    def _():
+        r = t - 5
+        dir_copy(r).wait()
+        rel_copy(r).wait()
+        parts = [[merged[r, chip, n] for n in range(tiles)], [dir_in[r, n] for n in range(tiles)], [rel_in[r, n] for n in range(tiles)]]
+        out, _, dens = merge_parts(parts, lane)
+        rows = [jnp.concatenate([out[4 * g + n] / dens[g] for n in range(rank // LANES)], axis=-1) for g in range(heads // SUBLANES)]
+        out_ref[r] = jnp.concatenate(rows, axis=0).astype(jnp.bfloat16)
+
+    @pl.when((t >= 3) & (t < rounds + 3))
+    def _():
+        rel_copy(t - 3).start()
+
+
+def attend_shards(positions, lat, rope_t, q_abs, q_rope, lat_new, rope_new, scale, n_tp, n_sp):
+    rows, slots, rank = lat.shape
+    heads, rope_dim = q_rope.shape[1:]
+    inner = rows // (n_tp * n_sp)
+    rounds = rows // n_sp
+    drain = 5
+    view = lambda a: a.reshape((n_tp, n_sp, inner) + a.shape[1:])
+
+    def block(*dims):
+        def index(t, pos):
+            r = jnp.minimum(t, rounds - 1)
+            return (r // inner, 0, lax.rem(r, inner)) + (0,) * len(dims)
+        return pl.BlockSpec((1, n_sp, 1) + dims, index)
+
+    whole = lambda a: pl.BlockSpec(a.shape, lambda t, pos: (0,) * a.ndim)
+    tiles = (heads // SUBLANES) * (rank // LANES) + 1
+    tile_set = (tiles, SUBLANES, LANES)
+    vmem = lambda *lead: pltpu.VMEM(lead + tile_set, jnp.float32)
+    sems = lambda n: pltpu.SemaphoreType.DMA((n,))
+    lat_new, rope_new = lat_new.astype(jnp.float32), rope_new.astype(jnp.float32)
+    return pl.pallas_call(
+        functools.partial(attend_kernel, rounds, inner, scale),
+        grid_spec=pltpu.PrefetchScalarGridSpec(
+            num_scalar_prefetch=1,
+            grid=(rounds + drain,),
+            in_specs=[block(slots, rank), block(rope_dim, slots), block(heads, rank), block(heads, rope_dim), whole(lat_new), whole(rope_new)],
+            out_specs=pl.BlockSpec((rounds, heads, rank), lambda t, pos: (0, 0, 0)),
+            scratch_shapes=[
+                vmem(rounds, 2, CHIPS), vmem(rounds, CHIPS), vmem(rounds, CHIPS), vmem(rounds), vmem(rounds), vmem(rounds), vmem(rounds),
+                sems(4), sems(4), sems(4), sems(4), sems(rounds), sems(rounds), sems(rounds), sems(rounds),
+            ],
+        ),
+        out_shape=jax.ShapeDtypeStruct((rounds, heads, rank), jnp.bfloat16),
+        compiler_params=pltpu.CompilerParams(collective_id=0, has_side_effects=True, vmem_limit_bytes=48 * 2 ** 20, dimension_semantics=('arbitrary',)),
+        name='attend',
+    )(positions, view(lat), view(rope_t), view(q_abs), view(q_rope), lat_new, rope_new)
+
+
 def solution(mesh):
     row_spec = P('dp', None)
     cache_spec = P('dp', 'sp', None)
     head_spec = P(None, 'tp', None)
     in_specs = (row_spec, cache_spec, cache_spec, P('dp'), P(), P(), P(), P(), head_spec, head_spec, head_spec, P('tp', None))
     out_specs = (row_spec, cache_spec, cache_spec)
+    n_tp, n_sp = mesh.shape['tp'], mesh.shape['sp']
 
     def local_step(hidden, lat_cache, rope_cache, positions, w_dq, gain_q, w_dkv, gain_kv, w_uq, w_uk, w_uv, w_out):
-        rows_local = hidden.shape[0]
         seq_local = lat_cache.shape[1]
         score_scale = YARN_MSCALE ** 2 / math.sqrt(w_uq.shape[2])
         q_abs, q_rope, lat_new, rope_new = project_inputs(hidden, positions, w_dq, gain_q, w_dkv, gain_kv, w_uq, w_uk)
+        rope_t = jnp.swapaxes(rope_cache, 1, 2)
+        o_lat = attend_shards(positions, lat_cache, rope_t, q_abs, q_rope, lat_new, rope_new, score_scale, n_tp, n_sp)
+        o_heads = jnp.einsum('bhk,khv->bhv', o_lat, w_uv, preferred_element_type=jnp.float32).astype(jnp.bfloat16)
+        attn_part = jnp.dot(o_heads.reshape(o_heads.shape[0], -1), w_out, preferred_element_type=jnp.float32)
+        attn_rows = lax.psum_scatter(attn_part, 'tp', scatter_dimension=0, tiled=True)
+        attn_out = lax.all_gather(attn_rows, ('tp', 'sp'), axis=0, tiled=True)
         slot_ids = lax.axis_index('sp') * seq_local + jnp.arange(seq_local)
         slot_hit = (slot_ids[None, :] == positions[:, None])[:, :, None]
         lat_all = jnp.where(slot_hit, lat_new[:, None, :], lat_cache)
         rope_all = jnp.where(slot_hit, rope_new[:, None, :], rope_cache)
-        scores = (jnp.einsum('bhk,bsk->bhs', q_abs, lat_all, preferred_element_type=jnp.float32) + jnp.einsum('bhr,bsr->bhs', q_rope, rope_all, preferred_element_type=jnp.float32)) * score_scale
-        key_valid = slot_ids[None, None, :] <= positions[:, None, None]
-        scores = jnp.where(key_valid, scores, MASK_VALUE)
-        max_global = lax.pmax(jnp.max(scores, axis=-1), 'sp')
-        weights = jnp.exp(scores - max_global[:, :, None])
-        lat_part = jnp.einsum('bhs,bsk->bhk', weights.astype(jnp.bfloat16), lat_all, preferred_element_type=jnp.float32)
-        denominator, lat_sum = lax.psum((jnp.sum(weights, axis=-1), lat_part), 'sp')
-        o_lat = (lat_sum / denominator[:, :, None]).astype(jnp.bfloat16)
-        o_heads = jnp.einsum('bhk,khv->bhv', o_lat, w_uv, preferred_element_type=jnp.float32).astype(jnp.bfloat16)
-        attn_part = jnp.dot(o_heads.reshape(rows_local, -1), w_out, preferred_element_type=jnp.float32)
-        attn_out = lax.psum(attn_part, 'tp')
         return (hidden.astype(jnp.float32) + attn_out).astype(jnp.bfloat16), lat_all, rope_all
 
     return jax.shard_map(local_step, mesh=mesh, in_specs=in_specs, out_specs=out_specs, check_vma=False)

time: 470 us -> 216 us (0.46)
  waiting for transfers between devices: 213 us -> 23.7 us
  matrix products: 113 us -> 37.2 us
  Pallas kernels: 0 us -> 69.6 us
  blocking collectives: 50.1 us -> 0 us
  local copies, waits for them, and re-layouts: 14.8 us -> 7.41 us
    psum x2 -> x0, waiting for transfers between devices: 213 us -> none  [the longest x1 140 us: local_step(): attn_out = lax.psum(attn_part, 'tp')]
    pallas_call x0 -> x1, Pallas kernels: none -> 69.6 us  [attend_shards(): pl.pallas_call(functools.partial(attend_kernel, rounds, inner, scale), gr...]
    dot_general x4 -> x1, matrix products: 78.4 us -> 13 us  [local_step(): jnp.dot(o_heads.reshape(o_heads.shape[0], -1), w_out, preferred_element_t...]
    psum x1 -> x0, blocking collectives: 25.9 us -> none  [local_step(): denominator, lat_sum = lax.psum((jnp.sum(weights, axis=-1), lat_part), 'sp')]
    pmax x1 -> x0, blocking collectives: 24.2 us -> none  [local_step(): max_global = lax.pmax(jnp.max(scores, axis=-1), 'sp')]
    reduce_scatter x0 -> x1, waiting for transfers between devices: none -> 23.6 us  [local_step(): lax.psum_scatter(attn_part, 'tp', scatter_dimension=0, tiled=True)]
    dot_general x1 -> x0, local copies, waits for them, and re-layouts: 11.5 us -> none  [local_step(): jnp.einsum('bhs,bsk->bhk', weights.astype(jnp.bfloat16), lat_all, preferr...]
  transfers between devices with their start and end apart: 2 -> 2, of which waited for: 2 -> 1; matrix products, arithmetic and copies ran while one was open for 1% -> 24% of each run, Pallas kernels for 0% -> 0%
where the time goes in v1:
time: 216 us; the launch traced here: 215 us
  Pallas kernels  69.6 us (32%)
  other arithmetic  63 us (29%)
  matrix products  37.2 us (17%)
  waiting for transfers between devices  23.7 us (11%)
  between operations  14.4 us (7%)
  local copies, waits for them, and re-layouts  7.41 us (3%)
    pallas_call x1, Pallas kernels, attend_shards(): pl.pallas_call(functools.partial(attend_kernel, rounds, inner, scale), gr...  69.6 us
    select_n x1, other arithmetic, local_step(): lat_all = jnp.where(slot_hit, lat_new[:, None, :], lat_cache)  44.6 us
    reduce_scatter x1, waiting for transfers between devices, local_step(): lax.psum_scatter(attn_part, 'tp', scatter_dimension=0, tiled=True)  23.6 us
    dot_general x1, matrix products, local_step(): jnp.dot(o_heads.reshape(o_heads.shape[0], -1), w_out, preferred_element_t...  13 us
    dot_general x1, matrix products, project_inputs(): jnp.dot(hidden, w_dq, preferred_element_type=jnp.float32)  10.7 us
    select_n x1, other arithmetic, local_step(): rope_all = jnp.where(slot_hit, rope_new[:, None, :], rope_cache)  7.94 us
    dot_general x1, matrix products, project_inputs(): jnp.dot(hidden, w_dkv, preferred_element_type=jnp.float32)  7.63 us
    convert_element_type x1, other arithmetic, local_step(): (hidden.astype(jnp.float32) + attn_out).astype(jnp.bfloat16)  7.07 us
  transfers between devices with their start and end apart: 2, of which 1 were waited for; matrix products, arithmetic and copies ran while one was open for 24% of the time, Pallas kernels for 0%

profile of v1, /device:TPU:102, one launch (start us, length us, event | category | flops | bytes accessed | tf_op | source)
XLA Modules:
  0.0 215.4 jit_solution(8542934277548072041)
XLA Ops:
  7.2 0.0 copy-start
  7.2 0.1 reduce-scatter.2.cloned.1.call-start
  7.3 0.0 copy-start.3
  7.3 0.0 slice-start
  7.3 7.6 %convolution_convert_fusion.1 = bf16[256,576]{1,0:T(8,128)(2,1)S(1)} fusion(bf16[256,7168]{1,0:T(8,128)(2,1)} %param.12, bf16[7168,576]{0,1:T(8,128)(2,1)} %param.18), kind=kOutput, calls=%fused_computation.11 | convolution fusion | flops 2114076672 | bytes 12222464 | tf_op jit(solution)/shard_map/dot_general | solution.py:49
  15.0 0.1 fusion.14
  15.1 0.0 copy-done.3
  15.1 0.0 copy-start.4
  15.1 0.0 slice-start.1
  15.1 0.0 slice-start.2
  15.1 10.7 %multiply_reduce_fusion = (f32[256]{0:T(256)S(1)}, f32[256,1536]{1,0:T(8,128)S(1)}) fusion(bf16[256,7168]{1,0:T(8,128)(2,1)S(1)} %copy-done.3, bf16[7168,1536]{1,0:T(8,128)(2,1)} %param.16), kind=kOutput, calls=%fused_computation.10 | convolution fusion | flops 5638717440 | bytes 27264000 | tf_op jit(solution)/shard_map/dot_general | solution.py:44
  25.8 0.0 copy-done.4
  25.9 0.0 slice-done
  25.9 0.0 slice-done.1
  25.9 0.0 slice-done.2
  25.9 2.8 %fusion.11 = f32[256,3072]{0,1:S(1)} fusion(bf16[1536,3072]{0,1:T(8,128)(2,1)S(1)} %bitcast.30, f32[256,1536]{1,0:T(8,128)S(1)} %get-tuple-element.14, f32[1536]{0:T(1024)S(1)} %convert_element_type.77, f32[256]{0:T(256)S(1)} %add_rsqrt_fusion.1), kind=kOutput, calls=%fused_computation.16 | convolution fusion | flops 2417098752 | bytes 14162944
  28.8 0.2 convert_element_type.79
  29.0 0.1 slice_convert_fusion
  29.1 0.0 copy-done
  29.1 1.6 convert_bitcast_fusion
  30.7 0.0 copy-start.2
  30.7 4.4 %copy.38 = bf16[256,16,512]{2,1,0:T(8,128)(2,1)} copy(bf16[256,16,512]{2,0,1:T(8,128)(2,1)S(1)} %convert_bitcast_fusion) | data formatting | bytes 8388608 | tf_op jit(solution)/shard_map/convert_element_type | solution.py:48
  35.1 0.0 copy-done.2
  35.1 0.0 copy-start.5
  35.1 0.6 subtract_convert_fusion.1
  35.7 0.1 copy.41
  35.7 0.1 copy.40
  35.8 0.2 subtract_convert_fusion
  36.0 0.9 copy.43
  36.9 1.9 copy.42
  38.8 0.0 copy-done.5
  38.8 1.8 pad_maximum_fusion.qr_ref
  40.6 0.1 fusion.22
  40.8 0.1 fusion.21
  40.9 0.0 copy-start.6
  40.9 69.6 %attend.1 = bf16[32,16,512]{2,1,0:T(8,128)(2,1)S(1)} custom-call(s32[256]{0:T(256)S(1)} %copy-done.2, bf16[4,8,8,256,512]{4,3,2,1,0:T(8,128)(2,1)} %bitcast.lat_ref, bf16[4,8,8,64,256]{4,3,2,1,0:T(8,128)(2,1)} %bitcast.23, bf16[4,8,8,16,512]{4,3,2,1,0:T(8,128)(2,1)} %bitcast.24, bf16[4,8,8,16,64]{4,3,2,1,0:T(8,128)(2,1)S(1)} %pad_maximum_fusion.qr_ref, ...), custom_call_target="tpu_custom_call" | custom-call | tf_op jit(solution)/shard_map/attend/pallas_call | solution.py:232
  110.5 0.0 copy-done.6
  110.5 1.5 fusion.7
  112.0 13.0 %fusion.18 = f32[32,7168]{1,0:T(8,128)} fusion(bf16[2048,7168]{1,0:T(8,128)(2,1)} %param.23, bf16[16,4,8,128]{3,2,1,0:T(8,128)(2,1)S(1)} %fusion.7), kind=kOutput, calls=%fused_computation.30 | convolution fusion | flops 939524096 | bytes 30408704 | tf_op jit(solution)/shard_map/dot_general | solution.py:265
  125.0 0.1 reduce-scatter.2.cloned.1.call-update
  125.0 0.1 all-gather.2.cloned.1.call-start
  125.1 23.6 %reduce-scatter.2.cloned.1.call-done = f32[8,7168]{1,0:T(8,128)} async-done(((f32[32,7168]{1,0:T(8,128)}), f32[8,7168]{1,0:T(8,128)}) %reduce-scatter.2.cloned.1.call-update) | async-done | bytes 229392 | tf_op jit(solution)/shard_map/reduce_scatter | solution.py:266
  148.7 0.1 all-gather.2.cloned.1.call-update
  148.8 0.1 broadcast_compare_fusion
  148.9 7.9 %broadcast_select_fusion.1 = bf16[256,256,64]{1,2,0:T(8,128)(2,1)} fusion(bf16[256,256,64]{1,2,0:T(8,128)(2,1)} %param.14, pred[256,256]{1,0:T(8,128)(4,1)S(1)} %broadcast_compare_fusion, bf16[256,64]{1,0:T(8,128)(2,1)S(1)} %get-tuple-element.4), kind=kLoop, calls=%fused_computation.1 | loop fusion | flops 4194304 | bytes 16875520 | tf_op jit(solution)/shard_map/jit(_where)/select_n | solution.py:271
  156.9 44.6 %broadcast_select_fusion = bf16[256,256,512]{2,1,0:T(8,128)(2,1)} fusion(bf16[256,256,512]{2,1,0:T(8,128)(2,1)} %param.13, pred[256,256]{1,0:T(8,128)(4,1)S(1)} %broadcast_compare_fusion, bf16[256,512]{1,0:T(8,128)(2,1)S(1)} %get-tuple-element.6), kind=kLoop, calls=%fused_computation | loop fusion | flops 33554432 | bytes 134545408 | tf_op jit(solution)/shard_map/jit(_where)/select_n | solution.py:270
  201.4 0.0 all-gather.2.cloned.1.call-done
  201.4 0.0 copy-start.1
  201.4 7.1 %add_convert_fusion = bf16[256,7168]{1,0:T(8,128)(2,1)} fusion(f32[256,7168]{1,0:T(8,128)} %all-gather.2.cloned.1.call-done, bf16[256,7168]{1,0:T(8,128)(2,1)} %param.12), kind=kLoop, calls=%fused_computation.2 | loop fusion | flops 5505024 | bytes 14680064 | tf_op jit(solution)/shard_map/convert_element_type | solution.py:272
  208.5 0.0 copy-done.1
  (9 shorter events, 0.0 us)
Async XLA Ops:
  7.2 21.9 %copy-start = (bf16[512,16,128]{2,1,0:T(8,128)(2,1)S(1)}, bf16[512,16,128]{2,1,0:T(8,128)(2,1)}, u32[]{:S(2)}) copy-start(bf16[512,16,128]{2,1,0:T(8,128)(2,1)} %param.21) | copy-start | bytes 6291460
  7.2 141.5 %reduce-scatter.2.cloned.1.call-start = ((), (), s32[]{:S(2)}) async-start(), calls=%async_computation.1 | async-start | bytes 1146880 | tf_op jit(solution)/shard_map/reduce_scatter | solution.py:266
  7.3 7.8 %copy-start.3 = (bf16[256,7168]{1,0:T(8,128)(2,1)S(1)}, bf16[256,7168]{1,0:T(8,128)(2,1)}, u32[]{:S(2)}) copy-start(bf16[256,7168]{1,0:T(8,128)(2,1)} %param.12) | copy-start | bytes 11010052
  7.3 18.6 %slice-start = ((s8[9437184]{0:T(1024)(128)(4,1)}), s8[4194304]{0:T(1024)(128)(4,1)S(1)}, s32[]{:S(2)}) async-start(s8[9437184]{0:T(1024)(128)(4,1)} %bitcast.28), calls=%async_computation.3 | async-start | bytes 8388608
  15.1 10.7 %copy-start.4 = (bf16[1536]{0:T(1024)(128)(2,1)S(1)}, bf16[1536]{0:T(1024)(128)(2,1)}, u32[]{:S(2)}) copy-start(bf16[1536]{0:T(1024)(128)(2,1)} %param.17) | copy-start | bytes 9220
  15.1 10.8 %slice-start.1 = ((s8[9437184]{0:T(1024)(128)(4,1)}), s8[4194304]{0:T(1024)(128)(4,1)S(1)}, s32[]{:S(2)}) async-start(s8[9437184]{0:T(1024)(128)(4,1)} %bitcast.28), calls=%async_computation.4 | async-start | bytes 8388608
  15.1 10.8 %slice-start.2 = ((s8[9437184]{0:T(1024)(128)(4,1)}), s8[1048576]{0:T(1024)(128)(4,1)S(1)}, s32[]{:S(2)}) async-start(s8[9437184]{0:T(1024)(128)(4,1)} %bitcast.28), calls=%async_computation.5 | async-start | bytes 2097152
  30.7 4.4 %copy-start.2 = (s32[256]{0:T(256)S(1)}, s32[256]{0:T(256)}, u32[]{:S(2)}) copy-start(s32[256]{0:T(256)} %pos_ref.1) | copy-start | bytes 3076
  35.1 3.7 %copy-start.5 = (bf16[512]{0:T(512)(128)(2,1)S(1)}, bf16[512]{0:T(512)(128)(2,1)}, u32[]{:S(2)}) copy-start(bf16[512]{0:T(512)(128)(2,1)} %param.19) | copy-start | bytes 3076
  40.9 69.6 %copy-start.6 = (bf16[512,16,128]{2,1,0:T(8,128)(2,1)S(1)}, bf16[512,16,128]{2,1,0:T(8,128)(2,1)}, u32[]{:S(2)}) copy-start(bf16[512,16,128]{2,1,0:T(8,128)(2,1)} %param.22) | copy-start | bytes 6291460
  125.0 76.4 %all-gather.2.cloned.1.call-start = ((), (), s32[]{:S(2)}) async-start(), calls=%async_computation.2 | async-start | bytes 7569408 | tf_op jit(solution)/shard_map/all_gather | solution.py:267
  201.4 7.1 %copy-start.1 = (bf16[512,16,128]{2,1,0:T(8,128)(2,1)S(1)}, bf16[512,16,128]{2,1,0:T(8,128)(2,1)}, u32[]{:S(2)}) copy-start(bf16[512,16,128]{2,1,0:T(8,128)(2,1)} %param.21) | copy-start | bytes 6291460
Sparse Core Ops, SparseCore 0:
  125.1 23.5 reduce-scatter.1
  150.8 44.5 all-gather.1

commit v2 on v0

v2 whole, which is shorter than its diff:
```python
import functools
import math
import jax
import jax.numpy as jnp
from jax import lax
from jax.experimental import pallas as pl
from jax.experimental.pallas import tpu as pltpu
from jax.sharding import PartitionSpec as P

EPSILON = 1e-6
ROPE_BASE = 50000.0
YARN_MSCALE = 1.0 + 0.1 * math.log(32.0)
MASK_VALUE = -1e30
LAT_DEPTH = 5
CHIPS = 4
SUBLANES = 8
LANES = 128
NT_DIMS = (((1,), (1,)), ((), ()))


def rms_norm(values, gain):
    vals32 = values.astype(jnp.float32)
    inv_rms = lax.rsqrt(jnp.mean(vals32 * vals32, axis=-1, keepdims=True) + EPSILON)
    return vals32 * inv_rms * gain.astype(jnp.float32)


def rope_tables(positions, rope_dim):
    half_dim = rope_dim // 2
    inv_freq = ROPE_BASE ** (-jnp.arange(half_dim).astype(jnp.float32) / half_dim)
    angles = positions.astype(jnp.float32)[:, None] * inv_freq[None, :]
    return jnp.cos(angles), jnp.sin(angles)


def rotate_pairs(values, cos_t, sin_t):
    half_dim = values.shape[-1] // 2
    first_half = values[..., :half_dim]
    second_half = values[..., half_dim:]
    return jnp.concatenate([first_half * cos_t - second_half * sin_t, second_half * cos_t + first_half * sin_t], axis=-1)


def project_inputs(hidden, positions, w_dq, gain_q, w_dkv, gain_kv, w_uq, w_uk):
    kv_rank = w_uk.shape[0]
    nope_dim = w_uk.shape[2]
    cos_t, sin_t = rope_tables(positions, w_uq.shape[2] - nope_dim)
    h_q = jnp.dot(hidden, w_dq, preferred_element_type=jnp.float32).astype(jnp.bfloat16)
    c_q = rms_norm(h_q, gain_q).astype(jnp.bfloat16)
    q_full = jnp.einsum('br,rhd->bhd', c_q, w_uq, preferred_element_type=jnp.float32).astype(jnp.bfloat16)
    q_rope = rotate_pairs(q_full[:, :, nope_dim:].astype(jnp.float32), cos_t[:, None, :], sin_t[:, None, :]).astype(jnp.bfloat16)
    q_abs = jnp.einsum('bhn,khn->bhk', q_full[:, :, :nope_dim], w_uk, preferred_element_type=jnp.float32).astype(jnp.bfloat16)
    kv_down = jnp.dot(hidden, w_dkv, preferred_element_type=jnp.float32).astype(jnp.bfloat16)
    lat_new = rms_norm(kv_down[:, :kv_rank], gain_kv).astype(jnp.bfloat16)
    rope_new = rotate_pairs(kv_down[:, kv_rank:].astype(jnp.float32), cos_t, sin_t).astype(jnp.bfloat16)
    return q_abs, q_rope, lat_new, rope_new


def merge_parts(parts, lane):
    groups = len(parts[0]) // 4
    stats = [p[-1] for p in parts]
    out, maxes, dens = [], [], []
    for g in range(groups):
        ms = [jnp.broadcast_to(s[:, 2 * g:2 * g + 1], s.shape) for s in stats]
        ls = [jnp.broadcast_to(s[:, 2 * g + 1:2 * g + 2], s.shape) for s in stats]
        top = functools.reduce(jnp.maximum, ms)
        ws = [jnp.exp(m - top) for m in ms]
        maxes.append(top)
        dens.append(sum(w * l for w, l in zip(ws, ls)))
        for n in range(4):
            out.append(sum(w * p[4 * g + n] for w, p in zip(ws, parts)))
    return out, maxes, dens


def pack_stats(maxes, dens, lane):
    tile = jnp.zeros((SUBLANES, LANES), jnp.float32)
    for g, (m, l) in enumerate(zip(maxes, dens)):
        tile = jnp.where(lane == 2 * g, m, tile)
        tile = jnp.where(lane == 2 * g + 1, l, tile)
    return tile


def attend_kernel(rounds, inner, lags, scale, pos_ref, qa_ref, qr_ref, cn_ref, kn_ref, lat_ref, rope_ref, out_ref,
                  lat_buf, rope_buf, probs, new_probs, part, peer_in, merged, far_in, relay, dir_in, rel_in,
                  lat_sem, rope_sem, peer_send, far_send, dir_send, rel_send, peer_recv, far_recv, dir_recv, rel_recv):
    me = lax.axis_index('sp')
    chip, core = me // 2, lax.rem(me, 2)
    owners = lat_ref.shape[1]
    slots = lat_ref.shape[3]
    heads, rank = qa_ref.shape[3], qa_ref.shape[4]
    lane = lax.broadcasted_iota(jnp.int32, (SUBLANES, LANES), 1)
    tiles = part.shape[3]
    depth = lat_buf.shape[0]
    split = [slice(SUBLANES * g, SUBLANES * (g + 1)) for g in range(heads // SUBLANES)]
    lag_peer, lag_far, lag_last = lags

    def at_chip(index):
        return {'sp': lax.rem(index + CHIPS, CHIPS) * 2 + core}

    def direction(r):
        return 1 - 2 * lax.rem(r, 2)

    def remote(src, dst, send, recv, r, target):
        return pltpu.make_async_remote_copy(
            src_ref=src, dst_ref=dst.at[r], send_sem=send.at[lax.rem(r, send.shape[0])], recv_sem=recv.at[r],
            device_id=target, device_id_type=pl.DeviceIdType.MESH)

    def peer_copy(r):
        return remote(part.at[r, 1 - core], peer_in, peer_send, peer_recv, r, {'sp': chip * 2 + 1 - core})

    def far_copy(r):
        return remote(merged.at[r, lax.rem(chip + 2, CHIPS)], far_in, far_send, far_recv, r, at_chip(chip + direction(r)))

    def dir_copy(r):
        source = lax.rem(chip - direction(r) + CHIPS, CHIPS)
        return remote(merged.at[r, source], dir_in, dir_send, dir_recv, r, at_chip(chip - direction(r)))

    def rel_copy(r):
        return remote(relay.at[r], rel_in, rel_send, rel_recv, r, at_chip(chip + direction(r)))

    def lat_copy(r):
        slot = lax.rem(r, depth)
        return pltpu.make_async_copy(lat_ref.at[r // inner, :, lax.rem(r, inner)], lat_buf.at[slot], lat_sem.at[slot])

    def rope_copy(r):
        slot = lax.rem(r, depth)
        return pltpu.make_async_copy(rope_ref.at[r // inner, :, lax.rem(r, inner)], rope_buf.at[slot], rope_sem.at[slot])

    def fetch(r):
        lat_copy(r).start()
        rope_copy(r).start()

    def arrive(r):
        lat_copy(r).wait()
        rope_copy(r).wait()

    def row_of(r, j):
        return (r // inner) * (owners * inner) + j * inner + lax.rem(r, inner)

    def score(r, j):
        buf = lax.rem(r, depth)
        lat_s = lax.dot_general(qa_ref[r // inner, j, lax.rem(r, inner)], lat_buf[buf, j], NT_DIMS, preferred_element_type=jnp.float32)
        rope_s = jnp.dot(qr_ref[r // inner, j, lax.rem(r, inner)], rope_buf[buf, j], preferred_element_type=jnp.float32)
        return lat_s + rope_s

    def soften(r, j, raw):
        row = row_of(r, j)
        local = pos_ref[row] - me * slots
        slot = lax.broadcasted_iota(jnp.int32, (heads, slots), 1)
        qa, qr = qa_ref[r // inner, j, lax.rem(r, inner)], qr_ref[r // inner, j, lax.rem(r, inner)]
        s_new = (jnp.sum(qa.astype(jnp.float32) * cn_ref[pl.ds(row, 1), :], axis=-1, keepdims=True)
                 + jnp.sum(qr.astype(jnp.float32) * kn_ref[pl.ds(row, 1), :], axis=-1, keepdims=True)) * scale
        ok = slot < local
        hit = jnp.full((heads, 1), local, jnp.int32)
        hit = (hit >= 0) & (hit < slots)
        scores = jnp.where(ok, raw * scale, MASK_VALUE)
        s_new = jnp.where(hit, s_new, MASK_VALUE)
        top = jnp.maximum(jnp.max(scores, axis=-1, keepdims=True), s_new)
        weights = jnp.where(ok, jnp.exp(scores - top), 0.0)
        w_new = jnp.where(hit, jnp.exp(s_new - top), 0.0)
        den = jnp.sum(weights, axis=-1, keepdims=True) + w_new
        stats = pack_stats([top[g] for g in split], [den[g] for g in split], lane)
        return weights.astype(jnp.bfloat16), jnp.broadcast_to(w_new.astype(jnp.bfloat16).astype(jnp.float32), (heads, LANES)), stats

    def keep(r, soft):
        half = lax.rem(r, 2)
        for j, (weights, w_new, stats) in enumerate(soft):
            probs[half, j] = weights
            new_probs[half, j] = w_new
            part[r, j % 2, j // 2, tiles - 1] = stats

    def weigh(r, j):
        buf, half = lax.rem(r, depth), lax.rem(r, 2)
        lat_sum = jnp.dot(probs[half, j], lat_buf[buf, j], preferred_element_type=jnp.float32)
        w_new, c_new = new_probs[half, j], cn_ref[pl.ds(row_of(r, j), 1), :]
        for g in range(heads // SUBLANES):
            for n in range(rank // LANES):
                cols = slice(LANES * n, LANES * (n + 1))
                part[r, j % 2, j // 2, 4 * g + n] = lat_sum[split[g], cols] + w_new[split[g]] * c_new[:, cols]

    def put(dst, index, out, maxes, dens):
        for n in range(tiles - 1):
            dst[(*index, n)] = out[n]
        dst[(*index, tiles - 1)] = pack_stats(maxes, dens, lane)

    def merge_peer(r):
        for d in range(CHIPS):
            put(merged, (r, d), *merge_parts([[part[r, core, d, n] for n in range(tiles)], [peer_in[r, d, n] for n in range(tiles)]], lane))

    def merge_far(r):
        d = lax.rem(chip + direction(r) + CHIPS, CHIPS)
        put(relay, (r,), *merge_parts([[merged[r, d, n] for n in range(tiles)], [far_in[r, n] for n in range(tiles)]], lane))

    def merge_last(r):
        parts = [[merged[r, chip, n] for n in range(tiles)], [dir_in[r, n] for n in range(tiles)], [rel_in[r, n] for n in range(tiles)]]
        out, _, dens = merge_parts(parts, lane)
        rows = [jnp.concatenate([out[4 * g + n] / dens[g] for n in range(rank // LANES)], axis=-1) for g in range(heads // SUBLANES)]
        out_ref[r] = jnp.concatenate(rows, axis=0).astype(jnp.bfloat16)

    def start_sends(r):
        far_copy(r).start()
        dir_copy(r).start()

    def wait_last(r):
        dir_copy(r).wait()
        rel_copy(r).wait()

    for r in range(depth - 2):
        fetch(r)
    barrier = pltpu.get_barrier_semaphore()
    pl.semaphore_signal(barrier, inc=1, device_id={'sp': chip * 2 + 1 - core}, device_id_type=pl.DeviceIdType.MESH)
    pl.semaphore_signal(barrier, inc=1, device_id=at_chip(chip + 1), device_id_type=pl.DeviceIdType.MESH)
    pl.semaphore_signal(barrier, inc=1, device_id=at_chip(chip - 1), device_id_type=pl.DeviceIdType.MESH)
    pl.semaphore_wait(barrier, 3)

    def fetch_ahead(t):
        @pl.when(t < rounds - (depth - 2))
        def _():
            fetch(t + depth - 2)

    def edge_step(t, scoring):
        def stage(lag, *actions):
            @pl.when((t >= lag) & (t < rounds + lag))
            def _():
                for action in actions:
                    action(t - lag)

        if scoring:
            fetch_ahead(t)
            arrive(t)
            keep(t, [soften(t, j, score(t, j)) for j in range(owners)])
        stage(1, lambda r: [weigh(r, j) for j in range(owners)])
        stage(lag_peer, lambda r: peer_copy(r).wait(), merge_peer, start_sends)
        stage(lag_far, lambda r: far_copy(r).wait(), merge_far, lambda r: rel_copy(r).start())
        stage(lag_last, wait_last, merge_last)
        stage(1, lambda r: peer_copy(r).start())

    @pl.loop(0, lag_last)
    def _(t):
        edge_step(t, True)

    @pl.loop(lag_last, rounds)
    def _(t):
        fetch_ahead(t)
        arrive(t)
        peer_copy(t - lag_peer).wait()
        far_copy(t - lag_far).wait()
        wait_last(t - lag_last)
        merge_last(t - lag_last)
        merge_far(t - lag_far)
        merge_peer(t - lag_peer)
        raw = [score(t, j) for j in range(owners)]
        for j in range(owners):
            weigh(t - 1, j)
        keep(t, [soften(t, j, raw[j]) for j in range(owners)])
        start_sends(t - lag_peer)
        rel_copy(t - lag_far).start()
        peer_copy(t - 1).start()

    @pl.loop(rounds, rounds + lag_last)
    def _(t):
        edge_step(t, False)


def attend_shards(positions, lat, rope_t, q_abs, q_rope, lat_new, rope_new, scale, n_tp, n_sp):
    rows, slots, rank = lat.shape
    heads, rope_dim = q_rope.shape[1:]
    inner = rows // (n_tp * n_sp)
    rounds = rows // n_sp
    lags = (3, 7, 11)
    view = lambda a: a.reshape((n_tp, n_sp, inner) + a.shape[1:])

    tiles = (heads // SUBLANES) * (rank // LANES) + 1
    tile_set = (tiles, SUBLANES, LANES)
    vmem = lambda *lead: pltpu.VMEM(lead + tile_set, jnp.float32)
    sems = lambda n: pltpu.SemaphoreType.DMA((n,))
    lat_new, rope_new = lat_new.astype(jnp.float32), rope_new.astype(jnp.float32)
    return pl.pallas_call(
        functools.partial(attend_kernel, rounds, inner, lags, scale),
        in_specs=[pl.BlockSpec(memory_space=pltpu.SMEM)] + [pl.BlockSpec(memory_space=pltpu.VMEM)] * 4 + [pl.BlockSpec(memory_space=pl.ANY)] * 2,
        out_specs=pl.BlockSpec(memory_space=pltpu.VMEM),
        scratch_shapes=[
            pltpu.VMEM((LAT_DEPTH, n_sp, slots, rank), lat.dtype), pltpu.VMEM((LAT_DEPTH, n_sp, rope_dim, slots), rope_t.dtype),
            pltpu.VMEM((2, n_sp, heads, slots), jnp.bfloat16), pltpu.VMEM((2, n_sp, heads, LANES), jnp.float32),
            vmem(rounds, 2, CHIPS), vmem(rounds, CHIPS), vmem(rounds, CHIPS), vmem(rounds), vmem(rounds), vmem(rounds), vmem(rounds),
            sems(LAT_DEPTH), sems(LAT_DEPTH), sems(8), sems(8), sems(8), sems(8), sems(rounds), sems(rounds), sems(rounds), sems(rounds),
        ],
        out_shape=jax.ShapeDtypeStruct((rounds, heads, rank), jnp.bfloat16),
        compiler_params=pltpu.CompilerParams(collective_id=0, has_side_effects=True, vmem_limit_bytes=48 * 2 ** 20),
        name='attend',
    )(positions, view(q_abs), view(q_rope), lat_new, rope_new, view(lat), view(rope_t))


def project_kernel(chunks, cols, o_ref, w_ref, out_ref, w_buf, part, far_in, relay, dir_in, rel_in,
                   w_sem, far_send, dir_send, rel_send, far_recv, dir_recv, rel_recv):
    ring = CHIPS
    me = lax.axis_index('tp')
    depth = w_buf.shape[0]
    lag_far, lag_last = 2, 4

    def device(index):
        return {'tp': lax.rem(index + ring, ring)}

    def direction(n):
        return 1 - 2 * lax.rem(n, 2)

    def rows(index):
        return pl.ds(pl.multiple_of(lax.rem(index + ring, ring) * SUBLANES, SUBLANES), SUBLANES)

    def columns(n):
        return pl.ds(pl.multiple_of(n * cols, cols), cols)

    def remote(src, dst, send, recv, n, target):
        return pltpu.make_async_remote_copy(src_ref=src, dst_ref=dst.at[n], send_sem=send.at[n], recv_sem=recv.at[n],
                                            device_id=target, device_id_type=pl.DeviceIdType.MESH)

    def far_copy(n):
        return remote(part.at[n, rows(me + 2)], far_in, far_send, far_recv, n, device(me + direction(n)))

    def dir_copy(n):
        return remote(part.at[n, rows(me - direction(n))], dir_in, dir_send, dir_recv, n, device(me - direction(n)))

    def rel_copy(n):
        return remote(relay.at[n], rel_in, rel_send, rel_recv, n, device(me + direction(n)))

    def fetch(n):
        slot = lax.rem(n, depth)
        return pltpu.make_async_copy(w_ref.at[:, columns(n)], w_buf.at[slot], w_sem.at[slot])

    for n in range(depth - 1):
        fetch(n).start()
    barrier = pltpu.get_barrier_semaphore()
    pl.semaphore_signal(barrier, inc=1, device_id=device(me + 1), device_id_type=pl.DeviceIdType.MESH)
    pl.semaphore_signal(barrier, inc=1, device_id=device(me - 1), device_id_type=pl.DeviceIdType.MESH)
    pl.semaphore_wait(barrier, 2)

    @pl.loop(0, chunks + lag_last)
    def _(t):
        @pl.when(t < chunks - (depth - 1))
        def _():
            fetch(t + depth - 1).start()

        @pl.when(t < chunks)
        def _():
            fetch(t).wait()
            part[t] = jnp.dot(o_ref[...], w_buf[lax.rem(t, depth)], preferred_element_type=jnp.float32)

        @pl.when((t >= lag_last) & (t < chunks + lag_last))
        def _():
            n = t - lag_last
            dir_copy(n).wait()
            rel_copy(n).wait()
            out_ref[:, columns(n)] = part[n, rows(me)] + dir_in[n] + rel_in[n]

        @pl.when((t >= lag_far) & (t < chunks + lag_far))
        def _():
            n = t - lag_far
            far_copy(n).wait()
            relay[n] = part[n, rows(me + direction(n))] + far_in[n]

        @pl.when(t < chunks)
        def _():
            far_copy(t).start()
            dir_copy(t).start()

        @pl.when((t >= lag_far) & (t < chunks + lag_far))
        def _():
            rel_copy(t - lag_far).start()


def project_out(o_rows, w_out):
    rows, depth = o_rows.shape
    width = w_out.shape[1]
    cols = 1024
    chunks = width // cols
    block = lambda *lead: pltpu.VMEM(lead, jnp.float32)
    sems = pltpu.SemaphoreType.DMA((chunks,))
    return pl.pallas_call(
        functools.partial(project_kernel, chunks, cols),
        in_specs=[pl.BlockSpec(memory_space=pltpu.VMEM), pl.BlockSpec(memory_space=pl.ANY)],
        out_specs=pl.BlockSpec(memory_space=pltpu.VMEM),
        out_shape=jax.ShapeDtypeStruct((SUBLANES, width), jnp.float32),
        scratch_shapes=[
            pltpu.VMEM((4, depth, cols), w_out.dtype), block(chunks, rows, cols),
            block(chunks, SUBLANES, cols), block(chunks, SUBLANES, cols), block(chunks, SUBLANES, cols), block(chunks, SUBLANES, cols),
            pltpu.SemaphoreType.DMA((4,)), sems, sems, sems, sems, sems, sems,
        ],
        compiler_params=pltpu.CompilerParams(collective_id=1, has_side_effects=True, vmem_limit_bytes=28 * 2 ** 20),
        cost_estimate=pl.CostEstimate(flops=2 * rows * depth * width, bytes_accessed=2 * depth * width, transcendentals=0),
        name='project_out',
    )(o_rows, w_out)


def update_kernel(group, pos_ref, lat_ref, rope_ref, new_ref, col_ref, after_ref, lat_out, rope_out):
    first = pl.program_id(0) * group
    slots, rank = lat_ref.shape[1:]
    lat_out[...] = lat_ref[...]
    slot_row = lax.broadcasted_iota(jnp.int32, (16, rank), 0)
    slot_col = lax.broadcasted_iota(jnp.int32, rope_ref.shape[1:], 1)
    for j in range(group):
        local = pos_ref[first + j]
        start = pl.multiple_of(jnp.clip(local, 0, slots - 1) // 16 * 16, 16)
        window = lat_ref[j, pl.ds(start, 16), :].astype(jnp.float32)
        window = jnp.where(slot_row == local - start, new_ref[j:j + 1, :], window)
        lat_out[j, pl.ds(start, 16), :] = window.astype(lat_out.dtype)
        rope = jnp.where(slot_col == local, col_ref[0, :, j:j + 1], rope_ref[j].astype(jnp.float32))
        rope_out[j] = rope.astype(rope_out.dtype)


def update_caches(local_pos, lat, rope_t, lat_new, rope_new, after):
    rows, slots, rank = lat.shape
    rope_dim = rope_t.shape[1]
    group = 8
    cols = rope_new.reshape(rows // group, group, rope_dim).swapaxes(1, 2)
    lead = lambda *dims: pl.BlockSpec(dims, lambda i, pos: (i,) + (0,) * (len(dims) - 1))
    return pl.pallas_call(
        functools.partial(update_kernel, group),
        grid_spec=pltpu.PrefetchScalarGridSpec(
            num_scalar_prefetch=1,
            grid=(rows // group,),
            in_specs=[lead(group, slots, rank), lead(group, rope_dim, slots), lead(group, rank), lead(1, rope_dim, group), pl.BlockSpec(memory_space=pl.ANY)],
            out_specs=[lead(group, slots, rank), lead(group, rope_dim, slots)],
        ),
        out_shape=[jax.ShapeDtypeStruct(lat.shape, lat.dtype), jax.ShapeDtypeStruct(rope_t.shape, rope_t.dtype)],
        compiler_params=pltpu.CompilerParams(vmem_limit_bytes=60 * 2 ** 20, dimension_semantics=('arbitrary',)),
        cost_estimate=pl.CostEstimate(flops=50_000_000_000, bytes_accessed=4 * lat.size + 4 * rope_t.size, transcendentals=0),
        name='update_caches',
    )(local_pos, lat, rope_t, lat_new, cols, after)


def solution(mesh):
    row_spec = P('dp', None)
    cache_spec = P('dp', 'sp', None)
    head_spec = P(None, 'tp', None)
    in_specs = (row_spec, cache_spec, cache_spec, P('dp'), P(), P(), P(), P(), head_spec, head_spec, head_spec, P('tp', None))
    out_specs = (row_spec, cache_spec, cache_spec)
    n_tp, n_sp = mesh.shape['tp'], mesh.shape['sp']

    def local_step(hidden, lat_cache, rope_cache, positions, w_dq, gain_q, w_dkv, gain_kv, w_uq, w_uk, w_uv, w_out):
        seq_local = lat_cache.shape[1]
        score_scale = YARN_MSCALE ** 2 / math.sqrt(w_uq.shape[2])
        q_abs, q_rope, lat_new, rope_new = project_inputs(hidden, positions, w_dq, gain_q, w_dkv, gain_kv, w_uq, w_uk)
        rope_t = jnp.swapaxes(rope_cache, 1, 2)
        o_lat = attend_shards(positions, lat_cache, rope_t, q_abs, q_rope, lat_new, rope_new, score_scale, n_tp, n_sp)
        o_heads = jnp.einsum('bhk,khv->bhv', o_lat, w_uv, preferred_element_type=jnp.float32).astype(jnp.bfloat16)
        attn_rows = project_out(o_heads.reshape(o_heads.shape[0], -1), w_out)
        attn_out = lax.all_gather(attn_rows, ('tp', 'sp'), axis=0, tiled=True)
        local_pos = positions - lax.axis_index('sp') * seq_local
        lat_all, rope_all = update_caches(local_pos, lat_cache, rope_t, lat_new.astype(jnp.float32), rope_new.astype(jnp.float32), attn_rows)
        return (hidden.astype(jnp.float32) + attn_out).astype(jnp.bfloat16), lat_all, jnp.swapaxes(rope_all, 1, 2)

    return jax.shard_map(local_step, mesh=mesh, in_specs=in_specs, out_specs=out_specs, check_vma=False)
```

time: 470 us -> 211 us (0.45)
  waiting for transfers between devices: 213 us -> 0.06 us
  Pallas kernels: 0 us -> 144 us
  matrix products: 113 us -> 29.1 us
  other arithmetic: 63.4 us -> 11.1 us
  blocking collectives: 50.1 us -> 0 us
    psum x2 -> x0, waiting for transfers between devices: 213 us -> none  [the longest x1 140 us: local_step(): attn_out = lax.psum(attn_part, 'tp')]
    pallas_call x0 -> x3, Pallas kernels: none -> 144 us  [the longest x1 60.2 us: update_caches(): pl.pallas_call(functools.partial(update_kernel, group), grid_spec=pltpu.P...]
    dot_general x4 -> x0, matrix products: 78.4 us -> none  [the longest x1 28.2 us: local_step(): jnp.einsum('bhs,bsk->bhk', weights.astype(jnp.bfloat16), lat_all, preferr...]
    select_n x2 -> x0, other arithmetic: 52.5 us -> none  [the longest x1 44.6 us: local_step(): lat_all = jnp.where(slot_hit, lat_new[:, None, :], lat_cache)]
    psum x1 -> x0, blocking collectives: 25.9 us -> none  [local_step(): denominator, lat_sum = lax.psum((jnp.sum(weights, axis=-1), lat_part), 'sp')]
    pmax x1 -> x0, blocking collectives: 24.2 us -> none  [local_step(): max_global = lax.pmax(jnp.max(scores, axis=-1), 'sp')]
    dot_general x1 -> x0, local copies, waits for them, and re-layouts: 11.5 us -> none  [local_step(): jnp.einsum('bhs,bsk->bhk', weights.astype(jnp.bfloat16), lat_all, preferr...]
  transfers between devices with their start and end apart: 2 -> 1, of which waited for: 2 -> 0; matrix products, arithmetic and copies ran while one was open for 1% -> 1% of each run, Pallas kernels for 0% -> 29%
where the time goes in v2:
time: 211 us; the launch traced here: 210 us
  Pallas kernels  144 us (68%)
  matrix products  29.1 us (14%)
  between operations  14.3 us (7%)
  local copies, waits for them, and re-layouts  11.8 us (6%)
  other arithmetic  11.1 us (5%)
    pallas_call x1, Pallas kernels, update_caches(): pl.pallas_call(functools.partial(update_kernel, group), grid_spec=pltpu.P...  60.2 us
    pallas_call x1, Pallas kernels, attend_shards(): pl.pallas_call(functools.partial(attend_kernel, rounds, inner, lags, scal...  58.9 us
    pallas_call x1, Pallas kernels, project_out(): pl.pallas_call(functools.partial(project_kernel, chunks, cols), in_specs=...  24.9 us
    dot_general x1, matrix products, project_inputs(): jnp.dot(hidden, w_dq, preferred_element_type=jnp.float32)  11.7 us
    dot_general x1, matrix products, project_inputs(): jnp.dot(hidden, w_dkv, preferred_element_type=jnp.float32)  7.61 us
    convert_element_type x1, other arithmetic, local_step(): (hidden.astype(jnp.float32) + attn_out).astype(jnp.bfloat16)  7.07 us
    unnamed x1, matrix products  5.43 us
    another operation x2, local copies, waits for them, and re-layouts  4.7 us
  transfers between devices with their start and end apart: 1, of which 0 were waited for; matrix products, arithmetic and copies ran while one was open for 1% of the time, Pallas kernels for 29%

profile of v2, /device:TPU:102, one launch (start us, length us, event | category | flops | bytes accessed | tf_op | source)
XLA Modules:
  0.0 210.4 jit_solution(12240244070586185316)
XLA Ops:
  7.2 0.0 copy-start
  7.2 0.1 all-gather.2.cloned.1.call-start
  7.3 0.0 copy-start.8
  7.3 0.0 copy-start.7
  7.3 0.0 copy-start.3
  7.3 7.6 %convolution_convert_fusion.1 = bf16[256,576]{1,0:T(8,128)(2,1)S(1)} fusion(bf16[256,7168]{1,0:T(8,128)(2,1)} %param.12, bf16[7168,576]{0,1:T(8,128)(2,1)} %param.18), kind=kOutput, calls=%fused_computation.9 | convolution fusion | flops 2114076672 | bytes 12222464 | tf_op jit(solution)/shard_map/dot_general | solution.py:50
  14.9 0.1 fusion.14
  15.1 0.0 copy-done.8
  15.1 0.0 copy-done.7
  15.1 0.0 copy-done.3
  15.2 0.5 broadcast_subtract_fusion
  15.7 1.2 subtract_convert_fusion.1
  16.9 0.1 copy.56
  17.0 0.1 copy.55
  17.0 11.7 %multiply_reduce_fusion = (f32[256]{0:T(256)S(1)}, f32[256,1536]{1,0:T(8,128)S(1)}) fusion(bf16[256,7168]{1,0:T(8,128)(2,1)} %param.12, bf16[7168,1536]{1,0:T(8,128)(2,1)} %param.16), kind=kOutput, calls=%fused_computation.8 | convolution fusion | flops 5638717440 | bytes 27264000 | tf_op jit(solution)/shard_map/dot_general | solution.py:45
  28.8 5.4 %fusion.11 = f32[256,3072]{0,1:S(1)} fusion(bf16[1536,3072]{0,1:T(8,128)(2,1)} %bitcast.36, f32[256,1536]{1,0:T(8,128)S(1)} %get-tuple-element.16, f32[1536]{0:T(1024)S(1)} %convert_element_type.76, f32[256]{0:T(256)S(1)} %add_rsqrt_fusion.1), kind=kOutput, calls=%fused_computation.14 | convolution fusion | flops 2417098752 | bytes 14162944
  34.2 0.2 convert_element_type.78
  34.5 0.0 copy-start.4
  34.5 1.1 copy-done.4
  35.6 0.1 slice_convert_fusion
  35.7 0.9 subtract_convert_fusion
  36.6 1.9 copy.57
  38.6 2.8 %copy.58 = bf16[256,16,32]{2,1,0:T(8,128)(2,1)} copy(bf16[256,16,32]{0,2,1:T(8,128)(2,1)} %get-tuple-element.8) | data formatting | bytes 524288 | tf_op jit(solution)/shard_map/convert.9
  41.4 0.0 copy-done
  41.4 2.8 %convert_bitcast_fusion = bf16[256,16,512]{2,0,1:T(8,128)(2,1)S(1)} fusion(bf16[512,16,128]{2,1,0:T(8,128)(2,1)S(1)} %copy-done, bf16[256,16,192]{0,2,1:T(8,128)(2,1)} %copy-done.4), kind=kOutput, calls=%fused_computation.1 | convolution fusion | flops 538968064 | bytes 7340032 | tf_op jit(solution)/shard_map/bhn,khn->bhk/dot_general | solution.py:49
  44.2 0.0 copy-start.6
  44.2 0.0 copy-start.5
  44.2 4.4 %copy.53 = bf16[256,16,512]{2,1,0:T(8,128)(2,1)} copy(bf16[256,16,512]{2,0,1:T(8,128)(2,1)S(1)} %convert_bitcast_fusion) | data formatting | bytes 8388608 | tf_op jit(solution)/shard_map/convert_element_type | solution.py:49
  48.6 0.1 fusion.18.cn_ref.new_ref
  48.7 0.0 copy-start.2
  48.7 0.0 copy-done.6
  48.7 0.1 maximum_convert_fusion.kn_ref
  48.8 0.0 copy-done.5
  48.8 0.6 pad_maximum_fusion.qr_ref
  49.4 0.0 copy-start.9
  49.4 58.9 %attend.1 = bf16[32,16,512]{2,1,0:T(8,128)(2,1)S(1)} custom-call(s32[256]{0:T(256)S(1)} %copy-done.3, bf16[4,8,8,16,512]{4,3,2,1,0:T(8,128)(2,1)} %bitcast.27, bf16[4,8,8,16,64]{4,3,2,1,0:T(8,128)(2,1)S(1)} %pad_maximum_fusion.qr_ref, f32[256,512]{1,0:T(8,128)S(1)} %fusion.18.cn_ref.new_ref, f32[256,64]{1,0:T(8,128)S(1)} %maximum_convert_fusion.kn_ref, ...), custom_call_target="tpu_custom_call" | custom-call | tf_op jit(solution)/shard_map/attend/pallas_call | solution.py:275
  108.3 0.0 copy-done.2
  108.4 0.0 copy-done.9
  108.4 1.5 fusion.7
  109.9 24.9 %project_out.1.after_ref = f32[8,7168]{1,0:T(8,128)} custom-call(bf16[32,2048]{1,0:T(8,128)(2,1)S(1)} %bitcast.26, bf16[2048,7168]{1,0:T(8,128)(2,1)} %w_ref.1), custom_call_target="tpu_custom_call" | custom-call | flops 939524096 | bytes 29360128 | tf_op jit(solution)/shard_map/project_out/pallas_call | solution.py:375
  134.8 0.1 all-gather.2.cloned.1.call-update
  134.9 0.1 maximum_convert_fusion.1
  135.0 1.3 copy.63
  136.3 60.2 %update_caches.1 = (bf16[256,256,512]{2,1,0:T(8,128)(2,1)}, bf16[256,64,256]{2,1,0:T(8,128)(2,1)}) custom-call(s32[256]{0:T(256)} %get-tuple-element.13.pos_ref, bf16[256,256,512]{2,1,0:T(8,128)(2,1)} %lat_ref.1, bf16[256,64,256]{2,1,0:T(8,128)(2,1)} %bitcast.29, f32[256,512]{1,0:T(8,128)} %copy-done.2, f32[32,64,8]{2,1,0:T(8,128)} %bitcast.33, ...), custom_call_target="tpu_custom_call" | custom-call | flops 49999998976 | bytes 150994944 | tf_op jit(solution)/shard_map/update_caches/pallas_call | solution.py:413
  196.5 0.0 all-gather.2.cloned.1.call-done
  196.5 0.0 copy-start.1
  196.5 7.1 %add_convert_fusion = bf16[256,7168]{1,0:T(8,128)(2,1)} fusion(f32[256,7168]{1,0:T(8,128)} %all-gather.2.cloned.1.call-done, bf16[256,7168]{1,0:T(8,128)(2,1)} %param.12), kind=kLoop, calls=%fused_computation | loop fusion | flops 5505024 | bytes 14680064 | tf_op jit(solution)/shard_map/convert_element_type | solution.py:447
  203.6 0.0 copy-done.1
  (7 shorter events, 0.1 us)
Async XLA Ops:
  7.2 34.2 %copy-start = (bf16[512,16,128]{2,1,0:T(8,128)(2,1)S(1)}, bf16[512,16,128]{2,1,0:T(8,128)(2,1)}, u32[]{:S(2)}) copy-start(bf16[512,16,128]{2,1,0:T(8,128)(2,1)} %param.21) | copy-start | bytes 6291460
  7.2 189.3 %all-gather.2.cloned.1.call-start = ((), (), s32[]{:S(2)}) async-start(), calls=%async_computation | async-start | bytes 7569408 | tf_op jit(solution)/shard_map/all_gather | solution.py:444
  7.3 7.8 %copy-start.8 = (bf16[512]{0:T(512)(128)(2,1)S(1)}, bf16[512]{0:T(512)(128)(2,1)}, u32[]{:S(2)}) copy-start(bf16[512]{0:T(512)(128)(2,1)} %param.19) | copy-start | bytes 3076
  7.3 7.8 %copy-start.7 = (bf16[1536]{0:T(1024)(128)(2,1)S(1)}, bf16[1536]{0:T(1024)(128)(2,1)}, u32[]{:S(2)}) copy-start(bf16[1536]{0:T(1024)(128)(2,1)} %param.17) | copy-start | bytes 9220
  7.3 7.8 %copy-start.3 = (s32[256]{0:T(256)S(1)}, s32[256]{0:T(256)}, u32[]{:S(2)}) copy-start(s32[256]{0:T(256)} %pos_ref.1) | copy-start | bytes 3076
  34.5 1.1 copy-start.4
  44.2 4.6 %copy-start.6 = (bf16[256,32]{1,0:T(8,128)(2,1)S(1)}, bf16[256,32]{1,0:T(8,128)(2,1)}, u32[]{:S(2)}) copy-start(bf16[256,32]{1,0:T(8,128)(2,1)} %get-tuple-element.10) | copy-start | bytes 49156
  44.2 4.7 %copy-start.5 = (bf16[256,16,32]{2,1,0:T(8,128)(2,1)S(1)}, bf16[256,16,32]{2,1,0:T(8,128)(2,1)}, u32[]{:S(2)}) copy-start(bf16[256,16,32]{2,1,0:T(8,128)(2,1)} %copy.58) | copy-start | bytes 786436
  48.7 59.6 %copy-start.2 = (f32[256,512]{1,0:T(8,128)}, f32[256,512]{1,0:T(8,128)S(1)}, u32[]{:S(2)}) copy-start(f32[256,512]{1,0:T(8,128)S(1)} %fusion.18.cn_ref.new_ref) | copy-start | bytes 1572868
  49.4 58.9 %copy-start.9 = (bf16[512,16,128]{2,1,0:T(8,128)(2,1)S(1)}, bf16[512,16,128]{2,1,0:T(8,128)(2,1)}, u32[]{:S(2)}) copy-start(bf16[512,16,128]{2,1,0:T(8,128)(2,1)} %param.22) | copy-start | bytes 6291460
  196.5 7.1 %copy-start.1 = (bf16[512,16,128]{2,1,0:T(8,128)(2,1)S(1)}, bf16[512,16,128]{2,1,0:T(8,128)(2,1)}, u32[]{:S(2)}) copy-start(bf16[512,16,128]{2,1,0:T(8,128)(2,1)} %param.21) | copy-start | bytes 6291460
Sparse Core Ops, SparseCore 0:
  135.0 43.3 all-gather.1

commit v3 on v2

--- a/solution.py
+++ b/solution.py
@@ -39,17 +39,14 @@
 
 
 def project_inputs(hidden, positions, w_dq, gain_q, w_dkv, gain_kv, w_uq, w_uk):
-    kv_rank = w_uk.shape[0]
     nope_dim = w_uk.shape[2]
     cos_t, sin_t = rope_tables(positions, w_uq.shape[2] - nope_dim)
-    h_q = jnp.dot(hidden, w_dq, preferred_element_type=jnp.float32).astype(jnp.bfloat16)
-    c_q = rms_norm(h_q, gain_q).astype(jnp.bfloat16)
+    c_q, lat_new, k_rope = project_down(hidden, w_dq, gain_q, w_dkv, gain_kv)
     q_full = jnp.einsum('br,rhd->bhd', c_q, w_uq, preferred_element_type=jnp.float32).astype(jnp.bfloat16)
     q_rope = rotate_pairs(q_full[:, :, nope_dim:].astype(jnp.float32), cos_t[:, None, :], sin_t[:, None, :]).astype(jnp.bfloat16)
+    q_rope = jnp.transpose(lax.optimization_barrier(jnp.transpose(q_rope, (1, 2, 0))), (2, 0, 1))
     q_abs = jnp.einsum('bhn,khn->bhk', q_full[:, :, :nope_dim], w_uk, preferred_element_type=jnp.float32).astype(jnp.bfloat16)
-    kv_down = jnp.dot(hidden, w_dkv, preferred_element_type=jnp.float32).astype(jnp.bfloat16)
-    lat_new = rms_norm(kv_down[:, :kv_rank], gain_kv).astype(jnp.bfloat16)
-    rope_new = rotate_pairs(kv_down[:, kv_rank:].astype(jnp.float32), cos_t, sin_t).astype(jnp.bfloat16)
+    rope_new = rotate_pairs(k_rope, cos_t, sin_t).astype(jnp.bfloat16)
     return q_abs, q_rope, lat_new, rope_new
 
 
@@ -271,7 +268,7 @@
     tile_set = (tiles, SUBLANES, LANES)
     vmem = lambda *lead: pltpu.VMEM(lead + tile_set, jnp.float32)
     sems = lambda n: pltpu.SemaphoreType.DMA((n,))
-    lat_new, rope_new = lat_new.astype(jnp.float32), rope_new.astype(jnp.float32)
+    rope_new = rope_new.astype(jnp.float32)
     return pl.pallas_call(
         functools.partial(attend_kernel, rounds, inner, lags, scale),
         in_specs=[pl.BlockSpec(memory_space=pltpu.SMEM)] + [pl.BlockSpec(memory_space=pltpu.VMEM)] * 4 + [pl.BlockSpec(memory_space=pl.ANY)] * 2,
@@ -388,41 +385,126 @@
     )(o_rows, w_out)
 
 
-def update_kernel(group, pos_ref, lat_ref, rope_ref, new_ref, col_ref, after_ref, lat_out, rope_out):
-    first = pl.program_id(0) * group
-    slots, rank = lat_ref.shape[1:]
-    lat_out[...] = lat_ref[...]
+def update_kernel(group, ahead, pos_ref, new_ref, col_ref, lat_ref, rope_ref, after_ref, lat_out, rope_out,
+                  lat_buf, rope_buf, lat_in_sem, rope_in_sem, lat_out_sem, rope_out_sem):
+    steps = lat_ref.shape[0] // group
+    depth, _, slots, rank = lat_buf.shape
     slot_row = lax.broadcasted_iota(jnp.int32, (16, rank), 0)
-    slot_col = lax.broadcasted_iota(jnp.int32, rope_ref.shape[1:], 1)
-    for j in range(group):
-        local = pos_ref[first + j]
-        start = pl.multiple_of(jnp.clip(local, 0, slots - 1) // 16 * 16, 16)
-        window = lat_ref[j, pl.ds(start, 16), :].astype(jnp.float32)
-        window = jnp.where(slot_row == local - start, new_ref[j:j + 1, :], window)
-        lat_out[j, pl.ds(start, 16), :] = window.astype(lat_out.dtype)
-        rope = jnp.where(slot_col == local, col_ref[0, :, j:j + 1], rope_ref[j].astype(jnp.float32))
-        rope_out[j] = rope.astype(rope_out.dtype)
+    slot_col = lax.broadcasted_iota(jnp.int32, rope_buf.shape[2:], 1)
+
+    def moves(i, inward):
+        slot, rows = lax.rem(i, depth), pl.ds(i * group, group)
+        if inward:
+            return (pltpu.make_async_copy(lat_ref.at[rows], lat_buf.at[slot], lat_in_sem.at[slot]),
+                    pltpu.make_async_copy(rope_ref.at[rows], rope_buf.at[slot], rope_in_sem.at[slot]))
+        return (pltpu.make_async_copy(lat_buf.at[slot], lat_out.at[rows], lat_out_sem.at[slot]),
+                pltpu.make_async_copy(rope_buf.at[slot], rope_out.at[rows], rope_out_sem.at[slot]))
+
+    def start(i, inward):
+        for move in moves(i, inward):
+            move.start()
+
+    def wait(i, inward):
+        for move in moves(i, inward):
+            move.wait()
+
+    for i in range(ahead):
+        start(i, True)
+
+    @pl.loop(0, steps)
+    def _(i):
+        @pl.when((i + ahead < steps) & (i + ahead >= depth))
+        def _():
+            wait(i + ahead - depth, False)
+
+        @pl.when(i + ahead < steps)
+        def _():
+            start(i + ahead, True)
+
+        wait(i, True)
+        slot = lax.rem(i, depth)
+        for j in range(group):
+            local = pos_ref[i * group + j]
+            first = pl.multiple_of(jnp.clip(local, 0, slots - 1) // 16 * 16, 16)
+            window = lat_buf[slot, j, pl.ds(first, 16), :].astype(jnp.float32)
+            window = jnp.where(slot_row == local - first, new_ref[pl.ds(i * group + j, 1), :], window)
+            lat_buf[slot, j, pl.ds(first, 16), :] = window.astype(lat_buf.dtype)
+            rope = jnp.where(slot_col == local, col_ref[i, :, j:j + 1], rope_buf[slot, j].astype(jnp.float32))
+            rope_buf[slot, j] = rope.astype(rope_buf.dtype)
+
+        @pl.when(i >= 1)
+        def _():
+            start(i - 1, False)
+
+    start(steps - 1, False)
+    for i in range(steps - depth, steps):
+        wait(i, False)
 
 
 def update_caches(local_pos, lat, rope_t, lat_new, rope_new, after):
     rows, slots, rank = lat.shape
     rope_dim = rope_t.shape[1]
-    group = 8
+    group, depth, ahead = 8, 14, 7
     cols = rope_new.reshape(rows // group, group, rope_dim).swapaxes(1, 2)
-    lead = lambda *dims: pl.BlockSpec(dims, lambda i, pos: (i,) + (0,) * (len(dims) - 1))
+    hbm = pl.BlockSpec(memory_space=pl.ANY)
+    vmem = pl.BlockSpec(memory_space=pltpu.VMEM)
+    sems = pltpu.SemaphoreType.DMA((depth,))
     return pl.pallas_call(
-        functools.partial(update_kernel, group),
-        grid_spec=pltpu.PrefetchScalarGridSpec(
-            num_scalar_prefetch=1,
-            grid=(rows // group,),
-            in_specs=[lead(group, slots, rank), lead(group, rope_dim, slots), lead(group, rank), lead(1, rope_dim, group), pl.BlockSpec(memory_space=pl.ANY)],
-            out_specs=[lead(group, slots, rank), lead(group, rope_dim, slots)],
-        ),
+        functools.partial(update_kernel, group, ahead),
+        in_specs=[pl.BlockSpec(memory_space=pltpu.SMEM), vmem, vmem, hbm, hbm, hbm],
+        out_specs=[hbm, hbm],
         out_shape=[jax.ShapeDtypeStruct(lat.shape, lat.dtype), jax.ShapeDtypeStruct(rope_t.shape, rope_t.dtype)],
-        compiler_params=pltpu.CompilerParams(vmem_limit_bytes=60 * 2 ** 20, dimension_semantics=('arbitrary',)),
+        scratch_shapes=[pltpu.VMEM((depth, group, slots, rank), lat.dtype), pltpu.VMEM((depth, group, rope_dim, slots), rope_t.dtype), sems, sems, sems, sems],
+        compiler_params=pltpu.CompilerParams(vmem_limit_bytes=60 * 2 ** 20),
         cost_estimate=pl.CostEstimate(flops=50_000_000_000, bytes_accessed=4 * lat.size + 4 * rope_t.size, transcendentals=0),
         name='update_caches',
-    )(local_pos, lat, rope_t, lat_new, cols, after)
+    )(local_pos, lat_new, cols, lat, rope_t, after)
+
+
+def down_kernel(x_ref, wq_ref, wkv_ref, gq_ref, gkv_ref, cq_ref, lat_ref, rope_ref, acc_q, acc_kv):
+    step = pl.program_id(0)
+    rank = gkv_ref.shape[1]
+    x = x_ref[...]
+    part_q = jnp.dot(x, wq_ref[...], preferred_element_type=jnp.float32)
+    part_kv = lax.dot_general(x, wkv_ref[...], NT_DIMS, preferred_element_type=jnp.float32)
+
+    @pl.when(step == 0)
+    def _():
+        acc_q[...] = part_q
+        acc_kv[...] = part_kv
+
+    @pl.when(step > 0)
+    def _():
+        acc_q[...] += part_q
+        acc_kv[...] += part_kv
+
+    @pl.when(step == pl.num_programs(0) - 1)
+    def _():
+        h_q = acc_q[...].astype(jnp.bfloat16)
+        cq_ref[...] = rms_norm(h_q, gq_ref[...]).astype(jnp.bfloat16)
+        kv = acc_kv[...].astype(jnp.bfloat16)
+        lat_ref[...] = rms_norm(kv[:, :rank], gkv_ref[...]).astype(jnp.bfloat16).astype(jnp.float32)
+        rope_ref[...] = kv[:, rank:].astype(jnp.float32)
+
+
+def project_down(hidden, w_dq, gain_q, w_dkv, gain_kv):
+    rows, model = hidden.shape
+    q_rank, kv_width, kv_rank = w_dq.shape[1], w_dkv.shape[1], gain_kv.shape[0]
+    span = 1792
+    whole = lambda *dims: pl.BlockSpec(dims, lambda k: (0,) * len(dims))
+    return pl.pallas_call(
+        down_kernel,
+        grid=(model // span,),
+        in_specs=[pl.BlockSpec((rows, span), lambda k: (0, k)), pl.BlockSpec((span, q_rank), lambda k: (k, 0)),
+                  pl.BlockSpec((kv_width, span), lambda k: (0, k)), whole(1, q_rank), whole(1, kv_rank)],
+        out_specs=[whole(rows, q_rank), whole(rows, kv_rank), whole(rows, kv_width - kv_rank)],
+        out_shape=[jax.ShapeDtypeStruct((rows, q_rank), jnp.bfloat16), jax.ShapeDtypeStruct((rows, kv_rank), jnp.float32),
+                   jax.ShapeDtypeStruct((rows, kv_width - kv_rank), jnp.float32)],
+        scratch_shapes=[pltpu.VMEM((rows, q_rank), jnp.float32), pltpu.VMEM((rows, kv_width), jnp.float32)],
+        compiler_params=pltpu.CompilerParams(vmem_limit_bytes=62 * 2 ** 20, dimension_semantics=('arbitrary',)),
+        cost_estimate=pl.CostEstimate(flops=2 * rows * model * (q_rank + kv_width), bytes_accessed=2 * model * (q_rank + kv_width), transcendentals=0),
+        name='project_down',
+    )(hidden, w_dq, jnp.swapaxes(w_dkv, 0, 1), gain_q[None, :], gain_kv[None, :])
 
 
 def solution(mesh):
@@ -443,7 +525,7 @@
         attn_rows = project_out(o_heads.reshape(o_heads.shape[0], -1), w_out)
         attn_out = lax.all_gather(attn_rows, ('tp', 'sp'), axis=0, tiled=True)
         local_pos = positions - lax.axis_index('sp') * seq_local
-        lat_all, rope_all = update_caches(local_pos, lat_cache, rope_t, lat_new.astype(jnp.float32), rope_new.astype(jnp.float32), attn_rows)
+        lat_all, rope_all = update_caches(local_pos, lat_cache, rope_t, lat_new, rope_new.astype(jnp.float32), attn_rows)
         return (hidden.astype(jnp.float32) + attn_out).astype(jnp.bfloat16), lat_all, jnp.swapaxes(rope_all, 1, 2)
 
     return jax.shard_map(local_step, mesh=mesh, in_specs=in_specs, out_specs=out_specs, check_vma=False)

time: 211 us -> 197 us (0.934)
  matrix products: 29.1 us -> 10.1 us
  Pallas kernels: 144 us -> 152 us
  local copies, waits for them, and re-layouts: 11.8 us -> 9.39 us
    dot_general x2 -> x0, matrix products: 19.4 us -> none  [the longest x1 11.7 us: project_inputs(): jnp.dot(hidden, w_dq, preferred_element_type=jnp.float32)]
    pallas_call x1 -> x2, Pallas kernels: 60.2 us -> 68 us  [the longest x1 50.6 us: update_caches(): pl.pallas_call(functools.partial(update_kernel, group, ahead), in_specs=[...]
    another operation x2 -> x0, local copies, waits for them, and re-layouts: 4.7 us -> none
    broadcast_in_dim x0 -> x2, local copies, waits for them, and re-layouts: none -> 2.54 us  [the longest x1 1.28 us: project_down(): gain_q[None, :]]
  transfers between devices with their start and end apart: 1 -> 1, of which waited for: 0 -> 0; matrix products, arithmetic and copies ran while one was open for 1% -> 1% of each run, Pallas kernels for 29% -> 26%
where the time goes in v3:
time: 197 us; the launch traced here: 196 us
  Pallas kernels  152 us (77%)
  between operations  14.2 us (7%)
  other arithmetic  10.5 us (5%)
  matrix products  10.1 us (5%)
  local copies, waits for them, and re-layouts  9.39 us (5%)
    pallas_call x1, Pallas kernels, attend_shards(): pl.pallas_call(functools.partial(attend_kernel, rounds, inner, lags, scal...  59.2 us
    pallas_call x1, Pallas kernels, update_caches(): pl.pallas_call(functools.partial(update_kernel, group, ahead), in_specs=[...  50.6 us
    pallas_call x1, Pallas kernels, project_out(): pl.pallas_call(functools.partial(project_kernel, chunks, cols), in_specs=...  24.9 us
    pallas_call x1, Pallas kernels, project_down(): pl.pallas_call(down_kernel, grid=(model // span,), in_specs=[pl.BlockSpec...  17.4 us
    convert_element_type x1, other arithmetic, local_step(): (hidden.astype(jnp.float32) + attn_out).astype(jnp.bfloat16)  6.92 us
    unnamed x1, matrix products  5.46 us
    convert_element_type x1, local copies, waits for them, and re-layouts, project_inputs(): jnp.einsum('bhn,khn->bhk', q_full[:, :, :nope_dim], w_uk, preferred_eleme...  4.38 us
  transfers between devices with their start and end apart: 1, of which 0 were waited for; matrix products, arithmetic and copies ran while one was open for 1% of the time, Pallas kernels for 26%

profile of v3, /device:TPU:102, one launch (start us, length us, event | category | flops | bytes accessed | tf_op | source)
XLA Modules:
  0.0 196.5 jit_solution(4410597143610059857)
XLA Ops:
  7.2 0.1 all-gather.2.cloned.1.call-start
  7.3 1.3 broadcast_in_dim.5.gkv_ref
  8.5 1.3 broadcast_in_dim.4.gq_ref
  9.8 1.3 broadcast_subtract_fusion
  11.1 17.4 %project_down.1 = (bf16[256,1536]{1,0:T(8,128)(2,1)}, f32[256,512]{1,0:T(8,128)}, f32[256,64]{1,0:T(8,128)}) custom-call(bf16[256,7168]{1,0:T(8,128)(2,1)} %x_ref.1, bf16[7168,1536]{1,0:T(8,128)(2,1)} %wq_ref.1, bf16[576,7168]{1,0:T(8,128)(2,1)} %bitcast.31, bf16[1,1536]{1,0:T(2,128)(2,1)} %broadcast_in_dim.4.gq_ref, bf16[1,512]{1,0:T(2,128)(2,1)} %broadcast_in_dim.5.gkv_ref), custom_call_target="tpu_custom_call" | custom-call | flops 7751073792 | bytes 30277632 | tf_op jit(solution)/shard_map/project_down/pallas_call | solution.py:495
  28.5 1.6 subtract_convert_fusion.1
  30.1 0.1 copy.50
  30.2 0.1 copy.49
  30.2 5.5 %fusion.11 = f32[256,3072]{0,1:S(1)} fusion(bf16[256,1536]{1,0:T(8,128)(2,1)} %get-tuple-element.8, bf16[1536,3072]{0,1:T(8,128)(2,1)} %bitcast.37), kind=kOutput, calls=%fused_computation.22 | convolution fusion | flops 2415919104 | bytes 13369344
  35.7 0.2 convert_element_type.42
  35.9 0.1 slice_convert_fusion
  36.0 0.2 subtract_convert_fusion
  36.2 1.0 copy.51
  37.2 3.1 %convert_bitcast_fusion = bf16[256,16,512]{2,0,1:T(8,128)(2,1)S(1)} fusion(bf16[512,16,128]{2,1,0:T(8,128)(2,1)} %param.21, bf16[256,16,192]{0,2,1:T(8,128)(2,1)S(1)} %convert_element_type.42), kind=kOutput, calls=%fused_computation.1 | convolution fusion | flops 538968064 | bytes 7340032 | tf_op jit(solution)/shard_map/bhn,khn->bhk/dot_general | solution.py:48
  40.3 0.0 copy-start
  40.3 0.0 copy-start.1
  40.3 4.4 %copy.47 = bf16[256,16,512]{2,1,0:T(8,128)(2,1)} copy(bf16[256,16,512]{2,0,1:T(8,128)(2,1)S(1)} %convert_bitcast_fusion) | data formatting | bytes 8388608 | tf_op jit(solution)/shard_map/convert_element_type | solution.py:48
  44.7 0.1 maximum_convert_fusion.kn_ref
  44.8 0.0 copy-done
  44.8 0.0 copy-done.1
  44.8 0.0 copy-start.2
  44.8 59.2 %attend.1 = bf16[32,16,512]{2,1,0:T(8,128)(2,1)S(1)} custom-call(s32[256]{0:T(256)S(1)} %copy-done.1, bf16[4,8,8,16,512]{4,3,2,1,0:T(8,128)(2,1)} %bitcast.28, bf16[4,8,8,16,64]{4,3,2,1,0:T(8,128)(2,1)S(1)} %bitcast.26, f32[256,512]{1,0:T(8,128)S(1)} %copy-done, f32[256,64]{1,0:T(8,128)S(1)} %maximum_convert_fusion.kn_ref, ...), custom_call_target="tpu_custom_call" | custom-call | tf_op jit(solution)/shard_map/attend/pallas_call | solution.py:272
  104.1 0.0 copy-done.2
  104.1 1.5 fusion.6
  105.6 24.9 %project_out.1.after_ref = f32[8,7168]{1,0:T(8,128)} custom-call(bf16[32,2048]{1,0:T(8,128)(2,1)S(1)} %bitcast.27, bf16[2048,7168]{1,0:T(8,128)(2,1)} %w_ref.1), custom_call_target="tpu_custom_call" | custom-call | flops 939524096 | bytes 29360128 | tf_op jit(solution)/shard_map/project_out/pallas_call | solution.py:372
  130.5 0.1 all-gather.2.cloned.1.call-update
  130.6 0.1 maximum_convert_fusion.1
  130.7 1.3 copy.55
  132.0 50.6 %update_caches.1 = (bf16[256,256,512]{2,1,0:T(8,128)(2,1)}, bf16[256,64,256]{2,1,0:T(8,128)(2,1)}) custom-call(s32[256]{0:T(256)} %get-tuple-element.19.pos_ref, f32[256,512]{1,0:T(8,128)} %get-tuple-element.9.cn_ref.new_ref, f32[32,64,8]{2,1,0:T(8,128)} %bitcast.34, bf16[256,256,512]{2,1,0:T(8,128)(2,1)} %lat_ref.1, bf16[256,64,256]{2,1,0:T(8,128)(2,1)} %bitcast.30, ...), custom_call_target="tpu_custom_call" | custom-call | flops 49999998976 | bytes 150994944 | tf_op jit(solution)/shard_map/update_caches/pallas_call | solution.py:452
  182.6 0.0 all-gather.2.cloned.1.call-done
  182.7 6.9 %add_convert_fusion = bf16[256,7168]{1,0:T(8,128)(2,1)} fusion(f32[256,7168]{1,0:T(8,128)} %all-gather.2.cloned.1.call-done, bf16[256,7168]{1,0:T(8,128)(2,1)} %x_ref.1), kind=kLoop, calls=%fused_computation | loop fusion | flops 5505024 | bytes 14680064 | tf_op jit(solution)/shard_map/convert_element_type | solution.py:529
  (3 shorter events, 0.1 us)
Async XLA Ops:
  7.2 175.5 %all-gather.2.cloned.1.call-start = ((), (), s32[]{:S(2)}) async-start(), calls=%async_computation | async-start | bytes 7569408 | tf_op jit(solution)/shard_map/all_gather | solution.py:526
  40.3 4.5 %copy-start = (f32[256,512]{1,0:T(8,128)S(1)}, f32[256,512]{1,0:T(8,128)}, u32[]{:S(2)}) copy-start(f32[256,512]{1,0:T(8,128)} %get-tuple-element.9.cn_ref.new_ref) | copy-start | bytes 1572868
  40.3 4.5 %copy-start.1 = (s32[256]{0:T(256)S(1)}, s32[256]{0:T(256)}, u32[]{:S(2)}) copy-start(s32[256]{0:T(256)} %pos_ref.1) | copy-start | bytes 3076
  44.8 59.3 %copy-start.2 = (bf16[512,16,128]{2,1,0:T(8,128)(2,1)S(1)}, bf16[512,16,128]{2,1,0:T(8,128)(2,1)}, u32[]{:S(2)}) copy-start(bf16[512,16,128]{2,1,0:T(8,128)(2,1)} %param.22) | copy-start | bytes 6291460
Sparse Core Ops, SparseCore 0:
  130.7 43.3 all-gather.1

commit v4 on v3

--- a/solution.py
+++ b/solution.py
@@ -261,7 +261,7 @@
     heads, rope_dim = q_rope.shape[1:]
     inner = rows // (n_tp * n_sp)
     rounds = rows // n_sp
-    lags = (3, 7, 11)
+    lags = (4, 9, 14)
     view = lambda a: a.reshape((n_tp, n_sp, inner) + a.shape[1:])
 
     tiles = (heads // SUBLANES) * (rank // LANES) + 1
@@ -461,9 +461,9 @@
     )(local_pos, lat_new, cols, lat, rope_t, after)
 
 
-def down_kernel(x_ref, wq_ref, wkv_ref, gq_ref, gkv_ref, cq_ref, lat_ref, rope_ref, acc_q, acc_kv):
+def down_kernel(x_ref, wq_ref, wkv_ref, gain_ref, cq_ref, lat_ref, rope_ref, acc_q, acc_kv):
     step = pl.program_id(0)
-    rank = gkv_ref.shape[1]
+    q_rank, rank = cq_ref.shape[1], lat_ref.shape[1]
     x = x_ref[...]
     part_q = jnp.dot(x, wq_ref[...], preferred_element_type=jnp.float32)
     part_kv = lax.dot_general(x, wkv_ref[...], NT_DIMS, preferred_element_type=jnp.float32)
@@ -481,9 +481,9 @@
     @pl.when(step == pl.num_programs(0) - 1)
     def _():
         h_q = acc_q[...].astype(jnp.bfloat16)
-        cq_ref[...] = rms_norm(h_q, gq_ref[...]).astype(jnp.bfloat16)
+        cq_ref[...] = rms_norm(h_q, gain_ref[:, :q_rank]).astype(jnp.bfloat16)
         kv = acc_kv[...].astype(jnp.bfloat16)
-        lat_ref[...] = rms_norm(kv[:, :rank], gkv_ref[...]).astype(jnp.bfloat16).astype(jnp.float32)
+        lat_ref[...] = rms_norm(kv[:, :rank], gain_ref[:, q_rank:]).astype(jnp.bfloat16).astype(jnp.float32)
         rope_ref[...] = kv[:, rank:].astype(jnp.float32)
 
 
@@ -496,7 +496,7 @@
         down_kernel,
         grid=(model // span,),
         in_specs=[pl.BlockSpec((rows, span), lambda k: (0, k)), pl.BlockSpec((span, q_rank), lambda k: (k, 0)),
-                  pl.BlockSpec((kv_width, span), lambda k: (0, k)), whole(1, q_rank), whole(1, kv_rank)],
+                  pl.BlockSpec((kv_width, span), lambda k: (0, k)), whole(1, q_rank + kv_rank)],
         out_specs=[whole(rows, q_rank), whole(rows, kv_rank), whole(rows, kv_width - kv_rank)],
         out_shape=[jax.ShapeDtypeStruct((rows, q_rank), jnp.bfloat16), jax.ShapeDtypeStruct((rows, kv_rank), jnp.float32),
                    jax.ShapeDtypeStruct((rows, kv_width - kv_rank), jnp.float32)],
@@ -504,7 +504,7 @@
         compiler_params=pltpu.CompilerParams(vmem_limit_bytes=62 * 2 ** 20, dimension_semantics=('arbitrary',)),
         cost_estimate=pl.CostEstimate(flops=2 * rows * model * (q_rank + kv_width), bytes_accessed=2 * model * (q_rank + kv_width), transcendentals=0),
         name='project_down',
-    )(hidden, w_dq, jnp.swapaxes(w_dkv, 0, 1), gain_q[None, :], gain_kv[None, :])
+    )(hidden, w_dq, jnp.swapaxes(w_dkv, 0, 1), jnp.concatenate([gain_q, gain_kv])[None, :])
 
 
 def solution(mesh):

time: 197 us -> 196 us (level)
  no operation moved by 1% of the time
where the time goes in v4:
time: 196 us; the launch traced here: 194 us
  Pallas kernels  151 us (77%)
  between operations  14.2 us (7%)
  other arithmetic  11.2 us (6%)
  matrix products  10.1 us (5%)
  local copies, waits for them, and re-layouts  7.45 us (4%)
    pallas_call x1, Pallas kernels, attend_shards(): pl.pallas_call(functools.partial(attend_kernel, rounds, inner, lags, scal...  58.6 us
    pallas_call x1, Pallas kernels, update_caches(): pl.pallas_call(functools.partial(update_kernel, group, ahead), in_specs=[...  50.6 us
    pallas_call x1, Pallas kernels, project_out(): pl.pallas_call(functools.partial(project_kernel, chunks, cols), in_specs=...  24.8 us
    pallas_call x1, Pallas kernels, project_down(): pl.pallas_call(down_kernel, grid=(model // span,), in_specs=[pl.BlockSpec...  17.4 us
    convert_element_type x1, other arithmetic, local_step(): (hidden.astype(jnp.float32) + attn_out).astype(jnp.bfloat16)  6.92 us
    unnamed x1, matrix products  5.46 us
    convert_element_type x1, local copies, waits for them, and re-layouts, project_inputs(): jnp.einsum('bhn,khn->bhk', q_full[:, :, :nope_dim], w_uk, preferred_eleme...  4.38 us
  transfers between devices with their start and end apart: 1, of which 0 were waited for; matrix products, arithmetic and copies ran while one was open for 1% of the time, Pallas kernels for 26%

profile of v4, /device:TPU:102, one launch (start us, length us, event | category | flops | bytes accessed | tf_op | source)
XLA Modules:
  0.0 194.5 jit_solution(5560523983501220693)
XLA Ops:
  7.2 0.1 all-gather.2.cloned.1.call-start
  7.3 0.7 pad_maximum_fusion
  8.0 0.6 broadcast_in_dim.2.gain_ref
  8.6 1.3 broadcast_subtract_fusion
  9.9 17.4 %project_down.1 = (bf16[256,1536]{1,0:T(8,128)(2,1)}, f32[256,512]{1,0:T(8,128)}, f32[256,64]{1,0:T(8,128)}) custom-call(bf16[256,7168]{1,0:T(8,128)(2,1)} %x_ref.1, bf16[7168,1536]{1,0:T(8,128)(2,1)} %wq_ref.1, bf16[576,7168]{1,0:T(8,128)(2,1)} %bitcast.31, bf16[1,2048]{1,0:T(2,128)(2,1)} %broadcast_in_dim.2.gain_ref), custom_call_target="tpu_custom_call" | custom-call | flops 7751073792 | bytes 30277632 | tf_op jit(solution)/shard_map/project_down/pallas_call | solution.py:495
  27.3 1.6 subtract_convert_fusion.1
  28.9 0.1 copy.50
  28.9 0.1 copy.49
  29.0 5.5 %fusion.11 = f32[256,3072]{0,1:S(1)} fusion(bf16[256,1536]{1,0:T(8,128)(2,1)} %get-tuple-element.8, bf16[1536,3072]{0,1:T(8,128)(2,1)} %bitcast.37), kind=kOutput, calls=%fused_computation.23 | convolution fusion | flops 2415919104 | bytes 13369344
  34.5 0.2 convert_element_type.42
  34.7 0.1 slice_convert_fusion
  34.8 0.2 subtract_convert_fusion
  35.0 1.0 copy.51
  36.0 3.1 %convert_bitcast_fusion = bf16[256,16,512]{2,0,1:T(8,128)(2,1)S(1)} fusion(bf16[512,16,128]{2,1,0:T(8,128)(2,1)} %param.21, bf16[256,16,192]{0,2,1:T(8,128)(2,1)S(1)} %convert_element_type.42), kind=kOutput, calls=%fused_computation.1 | convolution fusion | flops 538968064 | bytes 7340032 | tf_op jit(solution)/shard_map/bhn,khn->bhk/dot_general | solution.py:48
  39.1 0.0 copy-start
  39.1 0.0 copy-start.1
  39.1 4.4 %copy.47 = bf16[256,16,512]{2,1,0:T(8,128)(2,1)} copy(bf16[256,16,512]{2,0,1:T(8,128)(2,1)S(1)} %convert_bitcast_fusion) | data formatting | bytes 8388608 | tf_op jit(solution)/shard_map/convert_element_type | solution.py:48
  43.5 0.1 maximum_convert_fusion.kn_ref
  43.6 0.0 copy-done
  43.6 0.0 copy-done.1
  43.6 0.0 copy-start.2
  43.6 58.6 %attend.1 = bf16[32,16,512]{2,1,0:T(8,128)(2,1)S(1)} custom-call(s32[256]{0:T(256)S(1)} %copy-done.1, bf16[4,8,8,16,512]{4,3,2,1,0:T(8,128)(2,1)} %bitcast.28, bf16[4,8,8,16,64]{4,3,2,1,0:T(8,128)(2,1)S(1)} %bitcast.26, f32[256,512]{1,0:T(8,128)S(1)} %copy-done, f32[256,64]{1,0:T(8,128)S(1)} %maximum_convert_fusion.kn_ref, ...), custom_call_target="tpu_custom_call" | custom-call | tf_op jit(solution)/shard_map/attend/pallas_call | solution.py:272
  102.2 0.0 copy-done.2
  102.2 1.5 fusion.6
  103.7 24.8 %project_out.1.after_ref = f32[8,7168]{1,0:T(8,128)} custom-call(bf16[32,2048]{1,0:T(8,128)(2,1)S(1)} %bitcast.27, bf16[2048,7168]{1,0:T(8,128)(2,1)} %w_ref.1), custom_call_target="tpu_custom_call" | custom-call | flops 939524096 | bytes 29360128 | tf_op jit(solution)/shard_map/project_out/pallas_call | solution.py:372
  128.5 0.1 all-gather.2.cloned.1.call-update
  128.6 0.1 maximum_convert_fusion.1
  128.7 1.3 copy.55
  130.0 50.6 %update_caches.1 = (bf16[256,256,512]{2,1,0:T(8,128)(2,1)}, bf16[256,64,256]{2,1,0:T(8,128)(2,1)}) custom-call(s32[256]{0:T(256)} %get-tuple-element.19.pos_ref, f32[256,512]{1,0:T(8,128)} %get-tuple-element.9.cn_ref.new_ref, f32[32,64,8]{2,1,0:T(8,128)} %bitcast.34, bf16[256,256,512]{2,1,0:T(8,128)(2,1)} %lat_ref.1, bf16[256,64,256]{2,1,0:T(8,128)(2,1)} %bitcast.30, ...), custom_call_target="tpu_custom_call" | custom-call | flops 49999998976 | bytes 150994944 | tf_op jit(solution)/shard_map/update_caches/pallas_call | solution.py:452
  180.7 0.0 all-gather.2.cloned.1.call-done
  180.7 6.9 %add_convert_fusion = bf16[256,7168]{1,0:T(8,128)(2,1)} fusion(f32[256,7168]{1,0:T(8,128)} %all-gather.2.cloned.1.call-done, bf16[256,7168]{1,0:T(8,128)(2,1)} %x_ref.1), kind=kLoop, calls=%fused_computation | loop fusion | flops 5505024 | bytes 14680064 | tf_op jit(solution)/shard_map/convert_element_type | solution.py:529
  (3 shorter events, 0.1 us)
Async XLA Ops:
  7.2 173.5 %all-gather.2.cloned.1.call-start = ((), (), s32[]{:S(2)}) async-start(), calls=%async_computation | async-start | bytes 7569408 | tf_op jit(solution)/shard_map/all_gather | solution.py:526
  39.1 4.5 %copy-start = (f32[256,512]{1,0:T(8,128)S(1)}, f32[256,512]{1,0:T(8,128)}, u32[]{:S(2)}) copy-start(f32[256,512]{1,0:T(8,128)} %get-tuple-element.9.cn_ref.new_ref) | copy-start | bytes 1572868
  39.1 4.5 %copy-start.1 = (s32[256]{0:T(256)S(1)}, s32[256]{0:T(256)}, u32[]{:S(2)}) copy-start(s32[256]{0:T(256)} %pos_ref.1) | copy-start | bytes 3076
  43.6 58.6 %copy-start.2 = (bf16[512,16,128]{2,1,0:T(8,128)(2,1)S(1)}, bf16[512,16,128]{2,1,0:T(8,128)(2,1)}, u32[]{:S(2)}) copy-start(bf16[512,16,128]{2,1,0:T(8,128)(2,1)} %param.22) | copy-start | bytes 6291460
Sparse Core Ops, SparseCore 0:
  128.7 44.4 all-gather.1
